TPU v7x, 256 devices: a whole 4x4x8 slice. The times are simulated.
256 devices in a mesh: gx: 2 (over z_lo), gy: 16 (over x, y), gz: 8 (over z_hi, core).
Axes of the slice: x: 4, y: 4, z: 8 (z_hi: 4, z_lo: 2; z = z_hi * 2 + z_lo), core: 2. Of those that a mesh axis runs over, the one named last changes fastest.
Arguments:
- factors: bfloat16 [6144, 8, 4096], P('gy', None, 'gz'), may hold values from -0.046875 to 0.046875
- trial_vectors: float32 [64, 8, 4096], P('gx', None, 'gz'), may hold values from -6 to 6
- energy_gap: float32 [8, 4096], P(None, 'gz'), may hold values from 0.5 to 4
Outputs:
- updated_vectors: float32 [64, 8, 4096], P('gx', None, 'gz')
- coupling: float32 [64, 64], P(None, 'gx')
All inputs are finite; a program needn't handle non-finite values.
Results may differ from a plain program's by a relative error of at most 0.02.
Values may be sent and summed in bfloat16 or wider, within the bound.
No kernel may reach another device: no remote copies, remote signals or barrier semaphores. Data moves between devices by JAX's collectives and lax.ppermute only.
A program may use at most 64 MiB of HBM per device.

v0:
```python
import jax
import jax.numpy as jnp
from jax import lax
from jax.experimental import pallas as pl
from jax.experimental.pallas import tpu as pltpu
from jax.sharding import PartitionSpec as P

ITERS = 2
BF = jnp.bfloat16
F32 = jnp.float32
HIGHEST = lax.Precision.HIGHEST


NT = (((1,), (1,)), ((), ()))
NN = (((1,), (0,)), ((), ()))
TN = (((0,), (0,)), ((), ()))


def dot(a, b, dims, precision=None):
    return lax.dot_general(a, b, dims, precision=precision, preferred_element_type=F32)


SMEM = pl.BlockSpec(memory_space=pltpu.SMEM)
VMEM = pl.BlockSpec(memory_space=pltpu.VMEM)
PARAMS = pltpu.CompilerParams(vmem_limit_bytes=24 << 20)


def array(shape, dtype):
    return jax.ShapeDtypeStruct(shape, dtype)


def split(value):
    high = value.astype(BF).astype(F32)
    return high, value - high


def lanes(value, parts):
    rows = value.shape[0] // parts
    return jnp.concatenate([value[i * rows : (i + 1) * rows] for i in range(parts)], axis=1)


def unlanes(value, parts):
    width = value.shape[1] // parts
    return jnp.concatenate([value[:, i * width : (i + 1) * width] for i in range(parts)], axis=0)


def rows_of(steps, place, sibling):
    chip = place >> 1
    core = (1 - (place & 1)) if sibling else (place & 1)
    way = 2 * core - 1
    return [2 * ((chip + s * way) & 3) + core for s in steps]


def mix_kernel(place, x, b, *outs, sibling):
    rows = x.shape[1]
    order = rows_of((2, 1, -1, 0), place[2], sibling)
    chosen = jnp.concatenate([x[j] for j in order], axis=0)
    for r in range(b.shape[0]):
        part = dot(chosen, b[r], NT)
        for j in range(4):
            value = part[j * rows : (j + 1) * rows].astype(outs[0].dtype)
            if len(outs) == 1:
                outs[0][j, r * rows : (r + 1) * rows, :] = value
            else:
                outs[j][r * rows : (r + 1) * rows, :] = value


def mix(place, x, b, sibling, dtype, apart):
    r, k, _ = x.shape
    shape = (r * k, b.shape[1])
    outs = [array(shape, dtype)] * 4 if apart else [array((4, *shape), dtype)]
    return pl.pallas_call(
        lambda *refs: mix_kernel(*refs, sibling=sibling),
        out_shape=outs,
        in_specs=[SMEM, VMEM, VMEM],
        out_specs=[VMEM] * len(outs),
        compiler_params=PARAMS,
    )(place, x, b)


def gram_kernel(own, other, gap, out):
    r, k, _ = own.shape
    gram = jnp.zeros((2 * k, 2 * k), F32)
    scaled = jnp.zeros((2 * k, k), F32)
    for i in range(r):
        both = jnp.concatenate([own[i], other[i]], axis=0)
        gram += dot(both, both, NT)
        mine = own[i].astype(F32) * gap[i : i + 1, :]
        high, low = split(mine)
        scaled += dot(both, high.astype(BF), NT) + dot(both, low.astype(BF), NT)
    out[...] = jnp.concatenate([gram, scaled], axis=1)


def gram_parts(own, other, gap):
    k = own.shape[1]
    return pl.pallas_call(
        gram_kernel,
        out_shape=array((2 * k, 3 * k), F32),
        in_specs=[VMEM] * 3,
        out_specs=VMEM,
        compiler_params=PARAMS,
    )(own, other, gap)


def fock_kernel(place, *refs):
    blocks = refs[:8]
    b, own, other, gram, out, message, coulomb = refs[8:]
    r, k, _ = own.shape
    rows = r * k
    got = (0, -1, 1, 2)
    order = rows_of(got, place[2], False) + rows_of(got, place[2], True)
    fitted = jnp.zeros((k, b.shape[1]), F32)
    for j in range(8):
        start = pl.multiple_of(order[j] * k, k)
        fitted += blocks[j][pl.ds(start, k), :].astype(F32)
    fitted = fitted.astype(BF)
    total = jnp.zeros((rows, b.shape[2]), F32)
    for j in range(8):
        both = dot(jnp.concatenate([blocks[j][...], fitted], axis=0), b[order[j]], NN)
        total += both[:rows]
        coulomb[order[j]] = both[rows:]
    projected = jnp.zeros((2 * k, k), F32)
    for i in range(r):
        part = 2.0 * coulomb[i] - total[i * k : (i + 1) * k]
        part = part.astype(BF)
        out[i * k : (i + 1) * k, :] = part
        projected += dot(jnp.concatenate([own[i], other[i]], axis=0), part, NT)
    once = jnp.where(place[1] == 0, 1.0, 0.0)
    projected += once * gram[:, 2 * k :]
    message[...] = jnp.concatenate([lanes(gram[:, : 2 * k], 2), lanes(projected, 4)], axis=0)


def fock_parts(place, blocks, b, own, other, gram):
    r, k, n = own.shape
    return pl.pallas_call(
        fock_kernel,
        out_shape=(array((r * k, n), BF), array((3 * k // 2, 4 * k), F32)),
        in_specs=[SMEM] + [VMEM] * 12,
        out_specs=(VMEM, VMEM),
        scratch_shapes=[pltpu.VMEM((r, k, n), F32)],
        compiler_params=PARAMS,
    )(place, *blocks, b, own, other, gram)


def owner_kernel(arrived, s0, s1, s2, s3, out, totals):
    total = (s0[...] + s1[...]) + (s2[...] + s3[...])
    size = totals.shape[0]
    totals[...] = total[:size]
    high, low = split(total[size:])
    tail = jnp.concatenate([high, low], axis=0).astype(BF)
    fock = arrived[0].astype(F32)
    for j in range(1, arrived.shape[0]):
        fock += arrived[j].astype(F32)
    fock = fock.astype(BF)
    rows = fock.shape[0]
    for p in range(out.shape[0]):
        for i in range(4):
            out[p, i * rows : (i + 1) * rows, :] = fock[:, i * 128 : (i + 1) * 128]
        out[p, 4 * rows :, :] = tail


def owner_sums(arrived, sums, copies):
    rows = arrived.shape[1]
    k = 2 * sums[0].shape[0] // 3
    return pl.pallas_call(
        owner_kernel,
        out_shape=(array((copies, 4 * rows + k, 128), BF), array((k, 128), F32)),
        in_specs=[VMEM] * 5,
        out_specs=(VMEM, VMEM),
        compiler_params=PARAMS,
    )(arrived, *sums)


def inverse_kernel(totals, out):
    size = 2 * totals.shape[0]
    half = unlanes(totals[...], 2)
    rows = lax.broadcasted_iota(jnp.int32, (size, 2 * size), 0)
    columns = lax.broadcasted_iota(jnp.int32, (size, 2 * size), 1)
    identity = (columns == rows + size).astype(F32)
    work = jnp.concatenate([half, identity[:, size:]], axis=1)
    for j in range(0, size, 2):
        first, second = work[j : j + 1], work[j + 1 : j + 2]
        aa, ab, bb = first[:, j : j + 1], first[:, j + 1 : j + 2], second[:, j + 1 : j + 2]
        scale = 1.0 / (aa * bb - ab * ab)
        top = (bb * scale) * first - (ab * scale) * second
        bottom = (aa * scale) * second - (ab * scale) * first
        rest = work - work[:, j : j + 1] * top - work[:, j + 1 : j + 2] * bottom
        work = jnp.where(rows == j, top, jnp.where(rows == j + 1, bottom, rest))
    out[...] = work[:, size:]


def inverse_of(totals):
    size = 2 * totals.shape[0]
    return pl.pallas_call(
        inverse_kernel,
        out_shape=array((size, size), F32),
        in_specs=[VMEM],
        out_specs=VMEM,
        compiler_params=PARAMS,
    )(totals)


def solve(pieces, base, inverse, k, rows, swap=False):
    tail = jnp.zeros((k, 4 * k), F32)
    for j in range(16):
        tail += pieces[base + j, 4 * rows :, :].astype(F32)
    projected = unlanes(tail[: k // 2] + tail[k // 2 :], 4)
    if swap:
        projected = jnp.concatenate([projected[k:], projected[:k]], axis=0)
    return dot(inverse[...], projected, NN, HIGHEST)


def fock_rows(pieces, base, i, k, rows):
    per_row = k // rows
    parts = []
    for h in range(per_row):
        piece = pieces[base + i * per_row + h, : 4 * rows, :]
        parts.append(lanes(piece, 4))
    return jnp.concatenate(parts, axis=0).astype(F32)


def step_kernel(place, pieces, inverse, own, other, gap, own_out, other_out):
    r, k, _ = own.shape
    rows = (pieces.shape[1] - k) // 4
    bases = [16 * place[0], 16 * (1 - place[0])]
    mine = solve(pieces, bases[0], inverse, k, rows)
    theirs = solve(pieces, bases[1], inverse, k, rows, swap=True)
    high, low = split(jnp.concatenate([mine, theirs], axis=1))
    high, low = high.astype(BF), low.astype(BF)
    for i in range(r):
        both = jnp.concatenate([own[i], other[i]], axis=0)
        mixed = dot(high, both, TN) + dot(low, both, TN)
        inverse_gap = 1.0 / gap[i : i + 1, :]
        for out, base, part in zip((own_out, other_out), bases, (mixed[:k], mixed[k:])):
            out[i] = ((part - fock_rows(pieces, base, i, k, rows)) * inverse_gap).astype(BF)


def step_update(place, pieces, inverse, own, other, gap):
    return pl.pallas_call(
        step_kernel,
        out_shape=(array(own.shape, BF), array(own.shape, BF)),
        in_specs=[SMEM] + [VMEM] * 5,
        out_specs=(VMEM, VMEM),
        compiler_params=PARAMS,
    )(place, pieces, inverse, own, other, gap)


def last_kernel(place, pieces, inverse, own, other, gap, out, coupling):
    r, k, _ = own.shape
    rows = (pieces.shape[1] - k) // 4
    solved = solve(pieces, 0, inverse, k, rows)
    turned = solved.T
    swapped = jnp.concatenate([turned[:, k:], turned[:, :k]], axis=1)
    coupling[...] = jnp.where(place[0] == 0, turned, swapped)
    high, low = split(solved)
    high, low = high.astype(BF), low.astype(BF)
    for i in range(r):
        both = jnp.concatenate([own[i], other[i]], axis=0)
        mixed = dot(high, both, TN) + dot(low, both, TN)
        value = (mixed - fock_rows(pieces, 0, i, k, rows)) / gap[i : i + 1, :]
        out[:, i, :] = value


def last_update(place, pieces, inverse, own, other, gap):
    r, k, n = own.shape
    vectors, coupling = pl.pallas_call(
        last_kernel,
        out_shape=(array((k, r, n), F32), array((k, 2 * k), F32)),
        in_specs=[SMEM] + [VMEM] * 5,
        out_specs=(VMEM, VMEM),
        compiler_params=PARAMS,
    )(place, pieces, inverse, own, other, gap)
    return vectors, coupling.T


def ring(step):
    pairs = []
    for h in range(4):
        for c in range(2):
            way = step if c == 1 else -step
            pairs.append((2 * h + c, 2 * ((h + way) % 4) + c))
    return pairs


AHEAD = ring(1)
BACK = ring(-1)
SIBLING = [(i, i ^ 1) for i in range(8)]
OTHER = [(0, 1), (1, 0)]


def per_device(factors, trial_vectors, energy_gap):
    place = jnp.stack([lax.axis_index(a) for a in ("gx", "gy", "gz")])
    own = jnp.transpose(trial_vectors, (1, 0, 2)).astype(BF)
    other = lax.ppermute(own, "gx", OTHER)
    b = jnp.transpose(factors, (1, 0, 2))

    def add(*terms):
        return sum(t.astype(F32) for t in terms).astype(BF)

    def fock_sums(own, other):
        (theirs,) = mix(place, own, b, True, BF, False)
        theirs = lax.ppermute(theirs, "gz", SIBLING)
        mine = mix(place, own, b, False, F32, True)
        gram = gram_parts(own, other, energy_gap)
        far = lax.ppermute(add(mine[0], theirs[0]), "gz", AHEAD)
        near = lax.ppermute(add(mine[2], theirs[2]), "gz", BACK)
        far = lax.ppermute(add(mine[1], theirs[1], far), "gz", AHEAD)
        first = add(mine[3], theirs[3], near, far)
        second = lax.ppermute(first, "gz", AHEAD)
        third = lax.ppermute(first, "gz", BACK)
        fourth = lax.ppermute(second, "gz", AHEAD)
        blocks = [first, second, third, fourth]
        blocks += [lax.ppermute(a, "gz", SIBLING) for a in blocks]
        fock, sums = fock_parts(place, blocks, b, own, other, gram)
        arrived = lax.all_to_all(fock.reshape(16, -1, fock.shape[1]), "gy", 0, 0, tiled=True)
        sums = sums + lax.ppermute(sums, "gz", SIBLING)
        sums = [sums] + [
            lax.ppermute(sums, "gz", [(i, i ^ flip) for i in range(8)]) for flip in (2, 4, 6)
        ]
        return arrived, sums

    for iteration in range(ITERS):
        last = iteration == ITERS - 1
        arrived, sums = fock_sums(own, other)
        pieces, totals = owner_sums(arrived, sums, 16 if last else 32)
        axes = "gy" if last else ("gx", "gy")
        pieces = lax.all_to_all(pieces, axes, 0, 0, tiled=True)
        inverse = inverse_of(totals)
        if last:
            return last_update(place, pieces, inverse, own, other, energy_gap)
        own, other = step_update(place, pieces, inverse, own, other, energy_gap)


def solution(mesh):
    placed = (P("gy", None, "gz"), P("gx", None, "gz"), P(None, "gz"))
    return jax.shard_map(
        per_device,
        mesh=mesh,
        in_specs=placed,
        out_specs=(P("gx", None, "gz"), P(None, "gx")),
        check_vma=False,
    )
```

profile of v0, /device:TPU:2, one launch (start us, length us, event | category | flops | bytes accessed | tf_op | source)
XLA Modules:
  0.0 191.2 jit_solution(15076943619125944383)
XLA Ops:
  0.6 1.3 copy.12
  2.0 2.9 %copy.11 = bf16[384,8,512]{2,0,1:T(8,128)(2,1)S(1)} copy(bf16[384,8,512]{2,1,0:T(8,128)(2,1)} %param.3) | data formatting | bytes 6291456 | tf_op args[0]
  5.0 1.6 shard_map.51
  6.6 0.1 collective-permute-start
  6.7 1.6 shard_map.50
  8.3 0.7 collective-permute-done
  9.0 6.4 %collective-permute-start.2 = (bf16[256,384]{1,0:T(8,128)(2,1)S(1)}, bf16[256,384]{1,0:T(8,128)(2,1)S(1)}, u32[]{:S(2)}, u32[]{:S(2)}) collective-permute-start(bf16[256,384]{1,0:T(8,128)(2,1)S(1)} %get-tuple-element.45), channel_id=1, source_target_pairs={{0,6},{1,3},{2,0},{3,5},{4,2},{5,7},{6,4},{7,1},{8,14},{9,11},{10,... | collective-permute-start | bytes 589832 | tf_op jit(solution)/shard_map/ppermute | solution.py:305
  15.4 8.8 %collective-permute-done.2 = bf16[256,384]{1,0:T(8,128)(2,1)S(1)} collective-permute-done((bf16[256,384]{1,0:T(8,128)(2,1)S(1)}, bf16[256,384]{1,0:T(8,128)(2,1)S(1)}, u32[]{:S(2)}, u32[]{:S(2)}) %collective-permute-start.2) | collective-permute-done | bytes 196640 | tf_op jit(solution)/shard_map/ppermute | solution.py:305
  24.3 4.6 %collective-permute-start.3 = (bf16[256,384]{1,0:T(8,128)(2,1)S(1)}, bf16[256,384]{1,0:T(8,128)(2,1)S(1)}, u32[]{:S(2)}, u32[]{:S(2)}) collective-permute-start(bf16[256,384]{1,0:T(8,128)(2,1)S(1)} %fusion.9), channel_id=1, source_target_pairs={{0,6},{1,3},{2,0},{3,5},{4,2},{5,7},{6,4},{7,1},{8,14},{9,11},{10,... | collective-permute-start | bytes 589832 | tf_op jit(solution)/shard_map/ppermute | solution.py:307
  28.9 5.2 %collective-permute-done.3 = bf16[256,384]{1,0:T(8,128)(2,1)S(1)} collective-permute-done((bf16[256,384]{1,0:T(8,128)(2,1)S(1)}, bf16[256,384]{1,0:T(8,128)(2,1)S(1)}, u32[]{:S(2)}, u32[]{:S(2)}) %collective-permute-start.3) | collective-permute-done | bytes 196640 | tf_op jit(solution)/shard_map/ppermute | solution.py:307
  34.2 4.7 %collective-permute-start.4 = (bf16[256,384]{1,0:T(8,128)(2,1)S(1)}, bf16[256,384]{1,0:T(8,128)(2,1)S(1)}, u32[]{:S(2)}, u32[]{:S(2)}) collective-permute-start(bf16[256,384]{1,0:T(8,128)(2,1)S(1)} %fusion.13.refs_0_), channel_id=1, source_target_pairs={{0,6},{1,3},{2,0},{3,5},{4,2},{5,7},{6,4},{7,1},{8,14},{9,11},{10,... | collective-permute-start | bytes 589832 | tf_op jit(solution)/shard_map/ppermute | solution.py:309
  39.0 3.4 %collective-permute-done.4.refs_1_ = bf16[256,384]{1,0:T(8,128)(2,1)S(1)} collective-permute-done((bf16[256,384]{1,0:T(8,128)(2,1)S(1)}, bf16[256,384]{1,0:T(8,128)(2,1)S(1)}, u32[]{:S(2)}, u32[]{:S(2)}) %collective-permute-start.4) | collective-permute-done | bytes 196640 | tf_op jit(solution)/shard_map/ppermute | solution.py:309
  42.4 4.4 %collective-permute-start.6 = (bf16[256,384]{1,0:T(8,128)(2,1)S(1)}, bf16[256,384]{1,0:T(8,128)(2,1)S(1)}, u32[]{:S(2)}, u32[]{:S(2)}) collective-permute-start(bf16[256,384]{1,0:T(8,128)(2,1)S(1)} %collective-permute-done.4.refs_1_), channel_id=1, source_target_pairs={{0,6},{1,3},{2,0},{3,5},{4,2},{5,7},{6,4},{7,1},{8,14},{9,11},{10,... | collective-permute-start | bytes 589832 | tf_op jit(solution)/shard_map/ppermute | solution.py:311
  46.8 3.6 %collective-permute-start.11 = (bf16[8,32,512]{2,1,0:T(8,128)(2,1)S(1)}, bf16[8,32,512]{2,1,0:T(8,128)(2,1)S(1)}, u32[]{:S(2)}, u32[]{:S(2)}) collective-permute-start(bf16[8,32,512]{2,1,0:T(8,128)(2,1)S(1)} %bitcast.60), channel_id=1, source_target_pairs={{0,128},{128,0},{1,129},{129,1},{2,130},{130,2},{3,131},{131,3},{4... | collective-permute-start | bytes 786440 | tf_op jit(solution)/shard_map/ppermute | solution.py:294
  50.3 0.5 collective-permute-start.8
  50.9 2.7 %collective-permute-start.10 = (bf16[256,384]{1,0:T(8,128)(2,1)S(1)}, bf16[256,384]{1,0:T(8,128)(2,1)S(1)}, u32[]{:S(2)}, u32[]{:S(2)}) collective-permute-start(bf16[256,384]{1,0:T(8,128)(2,1)S(1)} %collective-permute-done.6.refs_3_), channel_id=1, source_target_pairs={{0,1},{1,0},{2,3},{3,2},{4,5},{5,4},{6,7},{7,6},{8,9},{9,8},{10,11... | collective-permute-start | bytes 589832 | tf_op jit(solution)/shard_map/ppermute | solution.py:313
  53.6 5.3 %collective-permute-done.11.other.refs_10_ = bf16[8,32,512]{2,1,0:T(8,128)(2,1)S(1)} collective-permute-done((bf16[8,32,512]{2,1,0:T(8,128)(2,1)S(1)}, bf16[8,32,512]{2,1,0:T(8,128)(2,1)S(1)}, u32[]{:S(2)}, u32[]{:S(2)}) %collective-permute-start.11) | collective-permute-done | bytes 262176 | tf_op jit(solution)/shard_map/ppermute | solution.py:294
  58.8 0.6 shard_map.52.refs_11_
  59.5 2.3 %shard_map.53 = (bf16[256,512]{1,0:T(8,128)(2,1)S(1)}, f32[48,128]{1,0:T(8,128)S(1)}) custom-call(s32[3]{0:T(128)S(1)} %pad_add_fusion.refs_0_.place, bf16[256,384]{1,0:T(8,128)(2,1)S(1)} %fusion.13.refs_0_, bf16[256,384]{1,0:T(8,128)(2,1)S(1)} %collective-permute-done.4.refs_1_, bf16[256,384]{1,0:T(8,128)(2,1)S(1)} %collective-permute-done.5.refs_2_, ...), custom_call_target="tpu_custom_call" | custom-call | tf_op jit(solution)/shard_map/pallas_call | solution.py:135
  61.8 0.7 copy-done.8
  62.5 7.5 %all-to-all-start = ((bf16[16,16,512]{2,1,0:T(8,128)(2,1)}), bf16[16,16,512]{2,1,0:T(8,128)(2,1)}, u32[]{:S(2)}, u32[]{:S(2)}) async-start(bf16[16,16,512]{2,1,0:T(8,128)(2,1)} %bitcast.64), calls=%async_computation | async-start | bytes 524288 | tf_op jit(solution)/shard_map/all_to_all | solution.py:315
  70.0 1.2 collective-permute-done.12
  71.2 2.9 %collective-permute-start.15 = (f32[48,128]{1,0:T(8,128)S(1)}, f32[48,128]{1,0:T(8,128)S(1)}, u32[]{:S(2)}, u32[]{:S(2)}) collective-permute-start(f32[48,128]{1,0:T(8,128)S(1)} %add.55.s0), channel_id=1, source_target_pairs={{0,6},{1,7},{2,4},{3,5},{4,2},{5,3},{6,0},{7,1},{8,14},{9,15},{10,... | collective-permute-start | bytes 73736 | tf_op jit(solution)/shard_map/ppermute | solution.py:318
  74.1 0.9 collective-permute-start.14
  75.0 2.7 %collective-permute-start.13 = (f32[48,128]{1,0:T(8,128)S(1)}, f32[48,128]{1,0:T(8,128)S(1)}, u32[]{:S(2)}, u32[]{:S(2)}) collective-permute-start(f32[48,128]{1,0:T(8,128)S(1)} %add.55.s0), channel_id=1, source_target_pairs={{0,2},{1,3},{2,0},{3,1},{4,6},{5,7},{6,4},{7,5},{8,10},{9,11},{10,... | collective-permute-start | bytes 73736 | tf_op jit(solution)/shard_map/ppermute | solution.py:318
  77.7 4.1 %collective-permute-done.14.s2 = f32[48,128]{1,0:T(8,128)S(1)} collective-permute-done((f32[48,128]{1,0:T(8,128)S(1)}, f32[48,128]{1,0:T(8,128)S(1)}, u32[]{:S(2)}, u32[]{:S(2)}) %collective-permute-start.14) | collective-permute-done | bytes 24608 | tf_op jit(solution)/shard_map/ppermute | solution.py:318
  81.8 1.0 shard_map.54
  82.9 0.9 copy-done.6
  83.7 7.4 %all-to-all-start.1 = ((bf16[32,96,128]{2,1,0:T(8,128)(2,1)}), bf16[32,96,128]{2,1,0:T(8,128)(2,1)}, u32[]{:S(2)}, u32[]{:S(2)}) async-start(bf16[32,96,128]{2,1,0:T(8,128)(2,1)} %copy-done.6), calls=%async_computation.1 | async-start | bytes 1572864 | tf_op jit(solution)/shard_map/all_to_all | solution.py:327
  91.2 7.4 %shard_map.55.inverse = f32[64,64]{1,0:T(8,128)S(1)} custom-call(f32[32,128]{1,0:T(8,128)S(1)} %get-tuple-element.29.totals), custom_call_target="tpu_custom_call" | custom-call | tf_op jit(solution)/shard_map/pallas_call | solution.py:194
  98.6 4.3 %all-to-all-done.1.pieces = bf16[32,96,128]{2,1,0:T(8,128)(2,1)} async-done(((bf16[32,96,128]{2,1,0:T(8,128)(2,1)}), bf16[32,96,128]{2,1,0:T(8,128)(2,1)}, u32[]{:S(2)}, u32[]{:S(2)}) %all-to-all-start.1) | async-done | bytes 786464 | tf_op jit(solution)/shard_map/all_to_all | solution.py:327
  102.9 0.9 copy-done.5
  103.8 1.9 %shard_map.56 = (bf16[8,32,512]{2,1,0:T(8,128)(2,1)S(1)}, bf16[8,32,512]{2,1,0:T(8,128)(2,1)S(1)}) custom-call(s32[3]{0:T(128)S(1)} %pad_add_fusion.refs_0_.place, bf16[32,96,128]{2,1,0:T(8,128)(2,1)} %all-to-all-done.1.pieces, f32[64,64]{1,0:T(8,128)S(1)} %shard_map.55.inverse, bf16[8,32,512]{2,1,0:T(8,128)(2,1)S(1)} %bitcast.63, ...), custom_call_target="tpu_custom_call" | custom-call | tf_op jit(solution)/shard_map/pallas_call | solution.py:239
  105.8 1.6 shard_map.58
  107.4 0.1 collective-permute-start.16
  107.5 1.6 shard_map.57
  109.1 0.7 collective-permute-done.16
  109.8 1.4 collective-permute-start.18
  111.2 1.6 collective-permute-start.17
  112.8 7.0 %collective-permute-done.18 = bf16[256,384]{1,0:T(8,128)(2,1)S(1)} collective-permute-done((bf16[256,384]{1,0:T(8,128)(2,1)S(1)}, bf16[256,384]{1,0:T(8,128)(2,1)S(1)}, u32[]{:S(2)}, u32[]{:S(2)}) %collective-permute-start.18) | collective-permute-done | bytes 196640 | tf_op jit(solution)/shard_map/ppermute | solution.py:305
  119.9 0.7 collective-permute-start.19
  120.6 2.6 %collective-permute-done.17 = bf16[256,384]{1,0:T(8,128)(2,1)S(1)} collective-permute-done((bf16[256,384]{1,0:T(8,128)(2,1)S(1)}, bf16[256,384]{1,0:T(8,128)(2,1)S(1)}, u32[]{:S(2)}, u32[]{:S(2)}) %collective-permute-start.17) | collective-permute-done | bytes 196640 | tf_op jit(solution)/shard_map/ppermute | solution.py:306
  123.2 3.3 %collective-permute-done.19 = bf16[256,384]{1,0:T(8,128)(2,1)S(1)} collective-permute-done((bf16[256,384]{1,0:T(8,128)(2,1)S(1)}, bf16[256,384]{1,0:T(8,128)(2,1)S(1)}, u32[]{:S(2)}, u32[]{:S(2)}) %collective-permute-start.19) | collective-permute-done | bytes 196640 | tf_op jit(solution)/shard_map/ppermute | solution.py:307
  126.7 1.9 %collective-permute-start.20 = (bf16[256,384]{1,0:T(8,128)(2,1)S(1)}, bf16[256,384]{1,0:T(8,128)(2,1)S(1)}, u32[]{:S(2)}, u32[]{:S(2)}) collective-permute-start(bf16[256,384]{1,0:T(8,128)(2,1)S(1)} %fusion.6.refs_0_), channel_id=1, source_target_pairs={{0,6},{1,3},{2,0},{3,5},{4,2},{5,7},{6,4},{7,1},{8,14},{9,11},{10,... | collective-permute-start | bytes 589832 | tf_op jit(solution)/shard_map/ppermute | solution.py:309
  128.6 1.1 collective-permute-start.21
  129.7 5.0 %collective-permute-done.20.refs_1_ = bf16[256,384]{1,0:T(8,128)(2,1)S(1)} collective-permute-done((bf16[256,384]{1,0:T(8,128)(2,1)S(1)}, bf16[256,384]{1,0:T(8,128)(2,1)S(1)}, u32[]{:S(2)}, u32[]{:S(2)}) %collective-permute-start.20) | collective-permute-done | bytes 196640 | tf_op jit(solution)/shard_map/ppermute | solution.py:309
  134.7 3.4 %collective-permute-start.22 = (bf16[256,384]{1,0:T(8,128)(2,1)S(1)}, bf16[256,384]{1,0:T(8,128)(2,1)S(1)}, u32[]{:S(2)}, u32[]{:S(2)}) collective-permute-start(bf16[256,384]{1,0:T(8,128)(2,1)S(1)} %collective-permute-done.20.refs_1_), channel_id=1, source_target_pairs={{0,6},{1,3},{2,0},{3,5},{4,2},{5,7},{6,4},{7,1},{8,14},{9,11},{10,... | collective-permute-start | bytes 589832 | tf_op jit(solution)/shard_map/ppermute | solution.py:311
  138.1 0.5 collective-permute-start.24
  138.6 4.4 %collective-permute-done.22.refs_3_ = bf16[256,384]{1,0:T(8,128)(2,1)S(1)} collective-permute-done((bf16[256,384]{1,0:T(8,128)(2,1)S(1)}, bf16[256,384]{1,0:T(8,128)(2,1)S(1)}, u32[]{:S(2)}, u32[]{:S(2)}) %collective-permute-start.22) | collective-permute-done | bytes 196640 | tf_op jit(solution)/shard_map/ppermute | solution.py:311
  143.1 0.6 shard_map.59.refs_11_
  143.7 0.8 collective-permute-done.26.refs_7_
  144.5 2.7 %shard_map.60 = (bf16[256,512]{1,0:T(8,128)(2,1)}, f32[48,128]{1,0:T(8,128)S(1)}) custom-call(s32[3]{0:T(128)S(1)} %pad_add_fusion.refs_0_.place, bf16[256,384]{1,0:T(8,128)(2,1)S(1)} %fusion.6.refs_0_, bf16[256,384]{1,0:T(8,128)(2,1)S(1)} %collective-permute-done.20.refs_1_, bf16[256,384]{1,0:T(8,128)(2,1)S(1)} %collective-permute-done.21.refs_2_, ...), custom_call_target="tpu_custom_call" | custom-call | tf_op jit(solution)/shard_map/pallas_call | solution.py:135
  147.3 11.0 %all-to-all-start.2 = ((bf16[16,16,512]{2,1,0:T(8,128)(2,1)}), bf16[16,16,512]{2,1,0:T(8,128)(2,1)S(1)}, u32[]{:S(2)}, u32[]{:S(2)}) async-start(bf16[16,16,512]{2,1,0:T(8,128)(2,1)} %bitcast.14), calls=%async_computation.2 | async-start | bytes 524288 | tf_op jit(solution)/shard_map/all_to_all | solution.py:315
  158.3 1.2 collective-permute-done.27
  159.5 3.5 %collective-permute-start.30 = (f32[48,128]{1,0:T(8,128)S(1)}, f32[48,128]{1,0:T(8,128)S(1)}, u32[]{:S(2)}, u32[]{:S(2)}) collective-permute-start(f32[48,128]{1,0:T(8,128)S(1)} %add.63.s0), channel_id=1, source_target_pairs={{0,6},{1,7},{2,4},{3,5},{4,2},{5,3},{6,0},{7,1},{8,14},{9,15},{10,... | collective-permute-start | bytes 73736 | tf_op jit(solution)/shard_map/ppermute | solution.py:318
  162.9 4.1 %collective-permute-start.29 = (f32[48,128]{1,0:T(8,128)S(1)}, f32[48,128]{1,0:T(8,128)S(1)}, u32[]{:S(2)}, u32[]{:S(2)}) collective-permute-start(f32[48,128]{1,0:T(8,128)S(1)} %add.63.s0), channel_id=1, source_target_pairs={{0,4},{1,5},{2,6},{3,7},{4,0},{5,1},{6,2},{7,3},{8,12},{9,13},{10,... | collective-permute-start | bytes 73736 | tf_op jit(solution)/shard_map/ppermute | solution.py:318
  167.1 3.9 %collective-permute-done.29.s2 = f32[48,128]{1,0:T(8,128)S(1)} collective-permute-done((f32[48,128]{1,0:T(8,128)S(1)}, f32[48,128]{1,0:T(8,128)S(1)}, u32[]{:S(2)}, u32[]{:S(2)}) %collective-permute-start.29) | collective-permute-done | bytes 24608 | tf_op jit(solution)/shard_map/ppermute | solution.py:318
  170.9 0.9 collective-permute-done.28.s1
  171.8 0.8 shard_map.61
  172.6 7.2 %all-to-all-start.3 = ((bf16[16,96,128]{2,1,0:T(8,128)(2,1)}), bf16[16,96,128]{2,1,0:T(8,128)(2,1)S(1)}, u32[]{:S(2)}, u32[]{:S(2)}) async-start(bf16[16,96,128]{2,1,0:T(8,128)(2,1)} %get-tuple-element.38), calls=%async_computation.3 | async-start | bytes 786432 | tf_op jit(solution)/shard_map/all_to_all | solution.py:327
  179.9 7.4 %shard_map.62.inverse = f32[64,64]{1,0:T(8,128)S(1)} custom-call(f32[32,128]{1,0:T(8,128)S(1)} %get-tuple-element.39.totals), custom_call_target="tpu_custom_call" | custom-call | tf_op jit(solution)/shard_map/pallas_call | solution.py:194
  187.3 1.0 copy-done.1
  188.3 0.9 copy-done.3
  189.2 2.0 %shard_map.63 = (f32[32,8,512]{2,1,0:T(8,128)}, f32[32,64]{1,0:T(8,128)}) custom-call(s32[3]{0:T(128)S(1)} %pad_add_fusion.refs_0_.place, bf16[16,96,128]{2,1,0:T(8,128)(2,1)S(1)} %all-to-all-done.3.pieces, f32[64,64]{1,0:T(8,128)S(1)} %shard_map.62.inverse, bf16[8,32,512]{2,1,0:T(8,128)(2,1)S(1)} %copy-done.1, bf16[8,32,512]{2,1,0:T(8,128)(2,1)S(1)} %copy-done.3, ...), custom_call_target="tpu_custom_call" | custom-call | tf_op jit(solution)/shard_map/pallas_call | solution.py:266
  (49 shorter events, 0.7 us)
Async XLA Ops:
  6.6 52.3 %copy-start.7 = (f32[8,512]{1,0:T(8,128)S(1)}, f32[8,512]{1,0:T(8,128)}, u32[]{:S(2)}) copy-start(f32[8,512]{1,0:T(8,128)} %gap.7) | copy-start | bytes 49156
  6.6 2.4 %collective-permute-start = (bf16[4,256,384]{2,1,0:T(8,128)(2,1)S(1)}, bf16[4,256,384]{2,1,0:T(8,128)(2,1)S(1)}, u32[]{:S(2)}, u32[]{:S(2)}) collective-permute-start(bf16[4,256,384]{2,1,0:T(8,128)(2,1)S(1)} %shard_map.51), channel_id=1, source_target_pairs={{0,1},{1,0},{2,3},{3,2},{4,5},{5,4},{6,7},{7,6},{8,9},{9,8},{10,11... | collective-permute-start | bytes 2359304 | tf_op jit(solution)/shard_map/ppermute | solution.py:302
  9.0 15.2 %collective-permute-start.2 = (bf16[256,384]{1,0:T(8,128)(2,1)S(1)}, bf16[256,384]{1,0:T(8,128)(2,1)S(1)}, u32[]{:S(2)}, u32[]{:S(2)}) collective-permute-start(bf16[256,384]{1,0:T(8,128)(2,1)S(1)} %get-tuple-element.45), channel_id=1, source_target_pairs={{0,6},{1,3},{2,0},{3,5},{4,2},{5,7},{6,4},{7,1},{8,14},{9,11},{10,... | collective-permute-start | bytes 589832 | tf_op jit(solution)/shard_map/ppermute | solution.py:305
  15.4 13.5 %collective-permute-start.1 = (bf16[256,384]{1,0:T(8,128)(2,1)S(1)}, bf16[256,384]{1,0:T(8,128)(2,1)S(1)}, u32[]{:S(2)}, u32[]{:S(2)}) collective-permute-start(bf16[256,384]{1,0:T(8,128)(2,1)S(1)} %get-tuple-element.44), channel_id=1, source_target_pairs={{0,2},{1,7},{2,4},{3,1},{4,6},{5,3},{6,0},{7,5},{8,10},{9,15},{10,... | collective-permute-start | bytes 589832 | tf_op jit(solution)/shard_map/ppermute | solution.py:306
  24.3 9.9 %collective-permute-start.3 = (bf16[256,384]{1,0:T(8,128)(2,1)S(1)}, bf16[256,384]{1,0:T(8,128)(2,1)S(1)}, u32[]{:S(2)}, u32[]{:S(2)}) collective-permute-start(bf16[256,384]{1,0:T(8,128)(2,1)S(1)} %fusion.9), channel_id=1, source_target_pairs={{0,6},{1,3},{2,0},{3,5},{4,2},{5,7},{6,4},{7,1},{8,14},{9,11},{10,... | collective-permute-start | bytes 589832 | tf_op jit(solution)/shard_map/ppermute | solution.py:307
  34.2 8.1 %collective-permute-start.4 = (bf16[256,384]{1,0:T(8,128)(2,1)S(1)}, bf16[256,384]{1,0:T(8,128)(2,1)S(1)}, u32[]{:S(2)}, u32[]{:S(2)}) collective-permute-start(bf16[256,384]{1,0:T(8,128)(2,1)S(1)} %fusion.13.refs_0_), channel_id=1, source_target_pairs={{0,6},{1,3},{2,0},{3,5},{4,2},{5,7},{6,4},{7,1},{8,14},{9,11},{10,... | collective-permute-start | bytes 589832 | tf_op jit(solution)/shard_map/ppermute | solution.py:309
  39.0 11.9 %collective-permute-start.5 = (bf16[256,384]{1,0:T(8,128)(2,1)S(1)}, bf16[256,384]{1,0:T(8,128)(2,1)S(1)}, u32[]{:S(2)}, u32[]{:S(2)}) collective-permute-start(bf16[256,384]{1,0:T(8,128)(2,1)S(1)} %fusion.13.refs_0_), channel_id=1, source_target_pairs={{0,2},{1,7},{2,4},{3,1},{4,6},{5,3},{6,0},{7,5},{8,10},{9,15},{10,... | collective-permute-start | bytes 589832 | tf_op jit(solution)/shard_map/ppermute | solution.py:310
  42.4 8.5 %collective-permute-start.6 = (bf16[256,384]{1,0:T(8,128)(2,1)S(1)}, bf16[256,384]{1,0:T(8,128)(2,1)S(1)}, u32[]{:S(2)}, u32[]{:S(2)}) collective-permute-start(bf16[256,384]{1,0:T(8,128)(2,1)S(1)} %collective-permute-done.4.refs_1_), channel_id=1, source_target_pairs={{0,6},{1,3},{2,0},{3,5},{4,2},{5,7},{6,4},{7,1},{8,14},{9,11},{10,... | collective-permute-start | bytes 589832 | tf_op jit(solution)/shard_map/ppermute | solution.py:311
  46.8 12.1 %collective-permute-start.11 = (bf16[8,32,512]{2,1,0:T(8,128)(2,1)S(1)}, bf16[8,32,512]{2,1,0:T(8,128)(2,1)S(1)}, u32[]{:S(2)}, u32[]{:S(2)}) collective-permute-start(bf16[8,32,512]{2,1,0:T(8,128)(2,1)S(1)} %bitcast.60), channel_id=1, source_target_pairs={{0,128},{128,0},{1,129},{129,1},{2,130},{130,2},{3,131},{131,3},{4... | collective-permute-start | bytes 786440 | tf_op jit(solution)/shard_map/ppermute | solution.py:294
  50.3 9.1 %collective-permute-start.7 = (bf16[256,384]{1,0:T(8,128)(2,1)S(1)}, bf16[256,384]{1,0:T(8,128)(2,1)S(1)}, u32[]{:S(2)}, u32[]{:S(2)}) collective-permute-start(bf16[256,384]{1,0:T(8,128)(2,1)S(1)} %fusion.13.refs_0_), channel_id=1, source_target_pairs={{0,1},{1,0},{2,3},{3,2},{4,5},{5,4},{6,7},{7,6},{8,9},{9,8},{10,11... | collective-permute-start | bytes 589832 | tf_op jit(solution)/shard_map/ppermute | solution.py:313
  50.3 9.1 %collective-permute-start.8 = (bf16[256,384]{1,0:T(8,128)(2,1)S(1)}, bf16[256,384]{1,0:T(8,128)(2,1)S(1)}, u32[]{:S(2)}, u32[]{:S(2)}) collective-permute-start(bf16[256,384]{1,0:T(8,128)(2,1)S(1)} %collective-permute-done.4.refs_1_), channel_id=1, source_target_pairs={{0,1},{1,0},{2,3},{3,2},{4,5},{5,4},{6,7},{7,6},{8,9},{9,8},{10,11... | collective-permute-start | bytes 589832 | tf_op jit(solution)/shard_map/ppermute | solution.py:313
  50.9 8.6 %collective-permute-start.9 = (bf16[256,384]{1,0:T(8,128)(2,1)S(1)}, bf16[256,384]{1,0:T(8,128)(2,1)S(1)}, u32[]{:S(2)}, u32[]{:S(2)}) collective-permute-start(bf16[256,384]{1,0:T(8,128)(2,1)S(1)} %collective-permute-done.5.refs_2_), channel_id=1, source_target_pairs={{0,1},{1,0},{2,3},{3,2},{4,5},{5,4},{6,7},{7,6},{8,9},{9,8},{10,11... | collective-permute-start | bytes 589832 | tf_op jit(solution)/shard_map/ppermute | solution.py:313
  50.9 8.6 %collective-permute-start.10 = (bf16[256,384]{1,0:T(8,128)(2,1)S(1)}, bf16[256,384]{1,0:T(8,128)(2,1)S(1)}, u32[]{:S(2)}, u32[]{:S(2)}) collective-permute-start(bf16[256,384]{1,0:T(8,128)(2,1)S(1)} %collective-permute-done.6.refs_3_), channel_id=1, source_target_pairs={{0,1},{1,0},{2,3},{3,2},{4,5},{5,4},{6,7},{7,6},{8,9},{9,8},{10,11... | collective-permute-start | bytes 589832 | tf_op jit(solution)/shard_map/ppermute | solution.py:313
  58.8 0.7 copy-start.4
  61.8 0.7 copy-start.8
  62.5 19.3 %all-to-all-start = ((bf16[16,16,512]{2,1,0:T(8,128)(2,1)}), bf16[16,16,512]{2,1,0:T(8,128)(2,1)}, u32[]{:S(2)}, u32[]{:S(2)}) async-start(bf16[16,16,512]{2,1,0:T(8,128)(2,1)} %bitcast.64), calls=%async_computation | async-start | bytes 524288 | tf_op jit(solution)/shard_map/all_to_all | solution.py:315
  70.0 1.2 collective-permute-start.12
  71.2 6.5 %collective-permute-start.15 = (f32[48,128]{1,0:T(8,128)S(1)}, f32[48,128]{1,0:T(8,128)S(1)}, u32[]{:S(2)}, u32[]{:S(2)}) collective-permute-start(f32[48,128]{1,0:T(8,128)S(1)} %add.55.s0), channel_id=1, source_target_pairs={{0,6},{1,7},{2,4},{3,5},{4,2},{5,3},{6,0},{7,1},{8,14},{9,15},{10,... | collective-permute-start | bytes 73736 | tf_op jit(solution)/shard_map/ppermute | solution.py:318
  74.1 7.7 %collective-permute-start.14 = (f32[48,128]{1,0:T(8,128)S(1)}, f32[48,128]{1,0:T(8,128)S(1)}, u32[]{:S(2)}, u32[]{:S(2)}) collective-permute-start(f32[48,128]{1,0:T(8,128)S(1)} %add.55.s0), channel_id=1, source_target_pairs={{0,4},{1,5},{2,6},{3,7},{4,0},{5,1},{6,2},{7,3},{8,12},{9,13},{10,... | collective-permute-start | bytes 73736 | tf_op jit(solution)/shard_map/ppermute | solution.py:318
  75.0 6.8 %collective-permute-start.13 = (f32[48,128]{1,0:T(8,128)S(1)}, f32[48,128]{1,0:T(8,128)S(1)}, u32[]{:S(2)}, u32[]{:S(2)}) collective-permute-start(f32[48,128]{1,0:T(8,128)S(1)} %add.55.s0), channel_id=1, source_target_pairs={{0,2},{1,3},{2,0},{3,1},{4,6},{5,7},{6,4},{7,5},{8,10},{9,11},{10,... | collective-permute-start | bytes 73736 | tf_op jit(solution)/shard_map/ppermute | solution.py:318
  82.9 0.9 copy-start.6
  83.7 19.1 %all-to-all-start.1 = ((bf16[32,96,128]{2,1,0:T(8,128)(2,1)}), bf16[32,96,128]{2,1,0:T(8,128)(2,1)}, u32[]{:S(2)}, u32[]{:S(2)}) async-start(bf16[32,96,128]{2,1,0:T(8,128)(2,1)} %copy-done.6), calls=%async_computation.1 | async-start | bytes 1572864 | tf_op jit(solution)/shard_map/all_to_all | solution.py:327
  102.9 1.0 copy-start.5
  105.8 38.7 %copy-start = (bf16[8,32,512]{2,1,0:T(8,128)(2,1)}, bf16[8,32,512]{2,1,0:T(8,128)(2,1)S(1)}, u32[]{:S(2)}) copy-start(bf16[8,32,512]{2,1,0:T(8,128)(2,1)S(1)} %get-tuple-element.30.refs_1_.own.refs_9_) | copy-start | bytes 786436
  105.8 38.7 %copy-start.2 = (bf16[8,32,512]{2,1,0:T(8,128)(2,1)}, bf16[8,32,512]{2,1,0:T(8,128)(2,1)S(1)}, u32[]{:S(2)}) copy-start(bf16[8,32,512]{2,1,0:T(8,128)(2,1)S(1)} %get-tuple-element.35.other.refs_10_) | copy-start | bytes 786436
  107.4 2.4 %collective-permute-start.16 = (bf16[4,256,384]{2,1,0:T(8,128)(2,1)S(1)}, bf16[4,256,384]{2,1,0:T(8,128)(2,1)S(1)}, u32[]{:S(2)}, u32[]{:S(2)}) collective-permute-start(bf16[4,256,384]{2,1,0:T(8,128)(2,1)S(1)} %shard_map.58), channel_id=1, source_target_pairs={{0,1},{1,0},{2,3},{3,2},{4,5},{5,4},{6,7},{7,6},{8,9},{9,8},{10,11... | collective-permute-start | bytes 2359304 | tf_op jit(solution)/shard_map/ppermute | solution.py:302
  109.8 10.0 %collective-permute-start.18 = (bf16[256,384]{1,0:T(8,128)(2,1)S(1)}, bf16[256,384]{1,0:T(8,128)(2,1)S(1)}, u32[]{:S(2)}, u32[]{:S(2)}) collective-permute-start(bf16[256,384]{1,0:T(8,128)(2,1)S(1)} %get-tuple-element.43), channel_id=1, source_target_pairs={{0,6},{1,3},{2,0},{3,5},{4,2},{5,7},{6,4},{7,1},{8,14},{9,11},{10,... | collective-permute-start | bytes 589832 | tf_op jit(solution)/shard_map/ppermute | solution.py:305
  111.2 12.0 %collective-permute-start.17 = (bf16[256,384]{1,0:T(8,128)(2,1)S(1)}, bf16[256,384]{1,0:T(8,128)(2,1)S(1)}, u32[]{:S(2)}, u32[]{:S(2)}) collective-permute-start(bf16[256,384]{1,0:T(8,128)(2,1)S(1)} %get-tuple-element.42), channel_id=1, source_target_pairs={{0,2},{1,7},{2,4},{3,1},{4,6},{5,3},{6,0},{7,5},{8,10},{9,15},{10,... | collective-permute-start | bytes 589832 | tf_op jit(solution)/shard_map/ppermute | solution.py:306
  119.9 6.6 %collective-permute-start.19 = (bf16[256,384]{1,0:T(8,128)(2,1)S(1)}, bf16[256,384]{1,0:T(8,128)(2,1)S(1)}, u32[]{:S(2)}, u32[]{:S(2)}) collective-permute-start(bf16[256,384]{1,0:T(8,128)(2,1)S(1)} %fusion.2), channel_id=1, source_target_pairs={{0,6},{1,3},{2,0},{3,5},{4,2},{5,7},{6,4},{7,1},{8,14},{9,11},{10,... | collective-permute-start | bytes 589832 | tf_op jit(solution)/shard_map/ppermute | solution.py:307
  126.7 8.0 %collective-permute-start.20 = (bf16[256,384]{1,0:T(8,128)(2,1)S(1)}, bf16[256,384]{1,0:T(8,128)(2,1)S(1)}, u32[]{:S(2)}, u32[]{:S(2)}) collective-permute-start(bf16[256,384]{1,0:T(8,128)(2,1)S(1)} %fusion.6.refs_0_), channel_id=1, source_target_pairs={{0,6},{1,3},{2,0},{3,5},{4,2},{5,7},{6,4},{7,1},{8,14},{9,11},{10,... | collective-permute-start | bytes 589832 | tf_op jit(solution)/shard_map/ppermute | solution.py:309
  128.6 10.1 %collective-permute-start.21 = (bf16[256,384]{1,0:T(8,128)(2,1)S(1)}, bf16[256,384]{1,0:T(8,128)(2,1)S(1)}, u32[]{:S(2)}, u32[]{:S(2)}) collective-permute-start(bf16[256,384]{1,0:T(8,128)(2,1)S(1)} %fusion.6.refs_0_), channel_id=1, source_target_pairs={{0,2},{1,7},{2,4},{3,1},{4,6},{5,3},{6,0},{7,5},{8,10},{9,15},{10,... | collective-permute-start | bytes 589832 | tf_op jit(solution)/shard_map/ppermute | solution.py:310
  134.7 8.4 %collective-permute-start.22 = (bf16[256,384]{1,0:T(8,128)(2,1)S(1)}, bf16[256,384]{1,0:T(8,128)(2,1)S(1)}, u32[]{:S(2)}, u32[]{:S(2)}) collective-permute-start(bf16[256,384]{1,0:T(8,128)(2,1)S(1)} %collective-permute-done.20.refs_1_), channel_id=1, source_target_pairs={{0,6},{1,3},{2,0},{3,5},{4,2},{5,7},{6,4},{7,1},{8,14},{9,11},{10,... | collective-permute-start | bytes 589832 | tf_op jit(solution)/shard_map/ppermute | solution.py:311
  138.1 5.6 %collective-permute-start.23 = (bf16[256,384]{1,0:T(8,128)(2,1)S(1)}, bf16[256,384]{1,0:T(8,128)(2,1)S(1)}, u32[]{:S(2)}, u32[]{:S(2)}) collective-permute-start(bf16[256,384]{1,0:T(8,128)(2,1)S(1)} %fusion.6.refs_0_), channel_id=1, source_target_pairs={{0,1},{1,0},{2,3},{3,2},{4,5},{5,4},{6,7},{7,6},{8,9},{9,8},{10,11... | collective-permute-start | bytes 589832 | tf_op jit(solution)/shard_map/ppermute | solution.py:313
  138.1 5.6 %collective-permute-start.24 = (bf16[256,384]{1,0:T(8,128)(2,1)S(1)}, bf16[256,384]{1,0:T(8,128)(2,1)S(1)}, u32[]{:S(2)}, u32[]{:S(2)}) collective-permute-start(bf16[256,384]{1,0:T(8,128)(2,1)S(1)} %collective-permute-done.20.refs_1_), channel_id=1, source_target_pairs={{0,1},{1,0},{2,3},{3,2},{4,5},{5,4},{6,7},{7,6},{8,9},{9,8},{10,11... | collective-permute-start | bytes 589832 | tf_op jit(solution)/shard_map/ppermute | solution.py:313
  138.6 5.1 %collective-permute-start.25 = (bf16[256,384]{1,0:T(8,128)(2,1)S(1)}, bf16[256,384]{1,0:T(8,128)(2,1)S(1)}, u32[]{:S(2)}, u32[]{:S(2)}) collective-permute-start(bf16[256,384]{1,0:T(8,128)(2,1)S(1)} %collective-permute-done.21.refs_2_), channel_id=1, source_target_pairs={{0,1},{1,0},{2,3},{3,2},{4,5},{5,4},{6,7},{7,6},{8,9},{9,8},{10,11... | collective-permute-start | bytes 589832 | tf_op jit(solution)/shard_map/ppermute | solution.py:313
  143.1 1.4 collective-permute-start.26
  147.3 24.6 %all-to-all-start.2 = ((bf16[16,16,512]{2,1,0:T(8,128)(2,1)}), bf16[16,16,512]{2,1,0:T(8,128)(2,1)S(1)}, u32[]{:S(2)}, u32[]{:S(2)}) async-start(bf16[16,16,512]{2,1,0:T(8,128)(2,1)} %bitcast.14), calls=%async_computation.2 | async-start | bytes 524288 | tf_op jit(solution)/shard_map/all_to_all | solution.py:315
  158.3 1.2 collective-permute-start.27
  159.5 7.6 %collective-permute-start.30 = (f32[48,128]{1,0:T(8,128)S(1)}, f32[48,128]{1,0:T(8,128)S(1)}, u32[]{:S(2)}, u32[]{:S(2)}) collective-permute-start(f32[48,128]{1,0:T(8,128)S(1)} %add.63.s0), channel_id=1, source_target_pairs={{0,6},{1,7},{2,4},{3,5},{4,2},{5,3},{6,0},{7,1},{8,14},{9,15},{10,... | collective-permute-start | bytes 73736 | tf_op jit(solution)/shard_map/ppermute | solution.py:318
  162.9 8.0 %collective-permute-start.29 = (f32[48,128]{1,0:T(8,128)S(1)}, f32[48,128]{1,0:T(8,128)S(1)}, u32[]{:S(2)}, u32[]{:S(2)}) collective-permute-start(f32[48,128]{1,0:T(8,128)S(1)} %add.63.s0), channel_id=1, source_target_pairs={{0,4},{1,5},{2,6},{3,7},{4,0},{5,1},{6,2},{7,3},{8,12},{9,13},{10,... | collective-permute-start | bytes 73736 | tf_op jit(solution)/shard_map/ppermute | solution.py:318
  167.1 4.8 %collective-permute-start.28 = (f32[48,128]{1,0:T(8,128)S(1)}, f32[48,128]{1,0:T(8,128)S(1)}, u32[]{:S(2)}, u32[]{:S(2)}) collective-permute-start(f32[48,128]{1,0:T(8,128)S(1)} %add.63.s0), channel_id=1, source_target_pairs={{0,2},{1,3},{2,0},{3,1},{4,6},{5,7},{6,4},{7,5},{8,10},{9,11},{10,... | collective-permute-start | bytes 73736 | tf_op jit(solution)/shard_map/ppermute | solution.py:318
  172.6 14.7 %all-to-all-start.3 = ((bf16[16,96,128]{2,1,0:T(8,128)(2,1)}), bf16[16,96,128]{2,1,0:T(8,128)(2,1)S(1)}, u32[]{:S(2)}, u32[]{:S(2)}) async-start(bf16[16,96,128]{2,1,0:T(8,128)(2,1)} %get-tuple-element.38), calls=%async_computation.3 | async-start | bytes 786432 | tf_op jit(solution)/shard_map/all_to_all | solution.py:327
  187.3 1.0 copy-start.1
  188.3 0.9 copy-start.3
where the time goes:
time: 192 us; the launch traced here: 191 us
  starting transfers between devices  85 us (44%)
  waiting for transfers between devices  62.8 us (33%)
  Pallas kernels  33.2 us (17%)
  local copies, waits for them, and re-layouts  8.75 us (5%)
    all_to_all x2, starting transfers between devices, fock_sums(): lax.all_to_all(fock.reshape(16, -1, fock.shape[1]), 'gy', 0, 0, tiled=True)  18.5 us
    ppermute x2, waiting for transfers between devices, fock_sums(): far = lax.ppermute(add(mine[0], theirs[0]), 'gz', AHEAD)  15.8 us
    pallas_call x2, Pallas kernels, inverse_of(): pl.pallas_call(inverse_kernel, out_shape=array((size, size), F32), in_spe...  14.9 us
    all_to_all x2, starting transfers between devices, per_device(): pieces = lax.all_to_all(pieces, axes, 0, 0, tiled=True)  14.6 us
    ppermute x6, starting transfers between devices, fock_sums(): lax.ppermute(sums, 'gz', [(i, i ^ flip) for i in range(8)])  14.1 us
    ppermute x6, waiting for transfers between devices, fock_sums(): lax.ppermute(sums, 'gz', [(i, i ^ flip) for i in range(8)])  8.87 us
    unnamed x20, local copies, waits for them, and re-layouts  8.75 us
    ppermute x2, waiting for transfers between devices, fock_sums(): far = lax.ppermute(add(mine[1], theirs[1], far), 'gz', AHEAD)  8.55 us
  transfers between devices with their start and end apart: 35, of which 18 were waited for; matrix products, arithmetic and copies ran while one was open for 0% of the time, Pallas kernels for 10%

commit v1 on v0

v1 whole, which is shorter than its diff:
```python
import jax
import jax.numpy as jnp
from jax import lax
from jax.experimental import pallas as pl
from jax.experimental.pallas import tpu as pltpu
from jax.sharding import PartitionSpec as P

ITERS = 2
BF = jnp.bfloat16
F32 = jnp.float32
HIGHEST = lax.Precision.HIGHEST


NT = (((1,), (1,)), ((), ()))
NN = (((1,), (0,)), ((), ()))
TN = (((0,), (0,)), ((), ()))


def dot(a, b, dims, precision=None):
    return lax.dot_general(a, b, dims, precision=precision, preferred_element_type=F32)


SMEM = pl.BlockSpec(memory_space=pltpu.SMEM)
VMEM = pl.BlockSpec(memory_space=pltpu.VMEM)
HBM = pl.BlockSpec(memory_space=pltpu.MemorySpace.HBM)
PARAMS = pltpu.CompilerParams(vmem_limit_bytes=24 << 20)


def array(shape, dtype):
    return jax.ShapeDtypeStruct(shape, dtype)


def split(value):
    high = value.astype(BF).astype(F32)
    return high, value - high


def lanes(value, parts):
    rows = value.shape[0] // parts
    return jnp.concatenate([value[i * rows : (i + 1) * rows] for i in range(parts)], axis=1)


def unlanes(value, parts):
    width = value.shape[1] // parts
    return jnp.concatenate([value[:, i * width : (i + 1) * width] for i in range(parts)], axis=0)


def rows_of(steps, place, sibling):
    chip = place >> 1
    core = (1 - (place & 1)) if sibling else (place & 1)
    way = 2 * core - 1
    return [2 * ((chip + s * way) & 3) + core for s in steps]


def fetch(source, order, buffer, arrivals):
    copies = [
        pltpu.make_async_copy(source.at[row], buffer.at[j], arrivals.at[j])
        for j, row in enumerate(order)
    ]
    for copy in copies:
        copy.start()
    return copies


def buffers(b):
    return [pltpu.VMEM(b.shape, b.dtype), pltpu.SemaphoreType.DMA((b.shape[0],))]


def mix_kernel(place, x, source, *refs, steps):
    *outs, b, arrivals = refs
    copies = fetch(source, range(source.shape[0]), b, arrivals)
    rows = x.shape[1]
    count = len(steps)
    order = rows_of(steps, place[2], True) + rows_of(steps, place[2], False)
    chosen = jnp.concatenate([x[j] for j in order], axis=0)
    for r in range(b.shape[0]):
        copies[r].wait()
        part = dot(chosen, b[r], NT)
        for j in range(count):
            theirs = part[j * rows : (j + 1) * rows]
            outs[0][j, r * rows : (r + 1) * rows, :] = theirs.astype(BF)
            mine = part[(count + j) * rows : (count + j + 1) * rows]
            outs[1 + j][r * rows : (r + 1) * rows, :] = mine


def mix(place, x, b, steps):
    r, k, _ = x.shape
    shape = (r * k, b.shape[1])
    outs = [array((len(steps), *shape), BF)] + [array(shape, F32)] * len(steps)
    return pl.pallas_call(
        lambda *refs: mix_kernel(*refs, steps=steps),
        out_shape=outs,
        in_specs=[SMEM, VMEM, HBM],
        out_specs=[VMEM] * len(outs),
        scratch_shapes=buffers(b),
        compiler_params=PARAMS,
    )(place, x, b)


def sums_kernel(place, own, other, gap, fock, message):
    r, k, _ = own.shape
    gram = jnp.zeros((2 * k, 2 * k), F32)
    scaled = jnp.zeros((2 * k, k), F32)
    projected = jnp.zeros((2 * k, k), F32)
    for i in range(r):
        both = jnp.concatenate([own[i], other[i]], axis=0)
        gram += dot(both, both, NT)
        high, low = split(own[i].astype(F32) * gap[i : i + 1, :])
        scaled += dot(both, high.astype(BF), NT) + dot(both, low.astype(BF), NT)
        projected += dot(both, fock[i * k : (i + 1) * k, :], NT)
    once = jnp.where(place[1] == 0, 1.0, 0.0)
    projected += once * scaled
    message[...] = jnp.concatenate([lanes(gram, 2), lanes(projected, 4)], axis=0)


def local_sums(place, own, other, gap, fock):
    k = own.shape[1]
    return pl.pallas_call(
        sums_kernel,
        out_shape=array((3 * k // 2, 4 * k), F32),
        in_specs=[SMEM] + [VMEM] * 4,
        out_specs=VMEM,
        compiler_params=PARAMS,
    )(place, own, other, gap, fock)


def fock_kernel(place, *refs):
    blocks = refs[:8]
    source, out, coulomb, b, arrivals = refs[8:]
    r, k, _ = coulomb.shape
    rows = r * k
    got = (0, -1, 1, 2)
    order = rows_of(got, place[2], False) + rows_of(got, place[2], True)
    copies = fetch(source, order, b, arrivals)
    fitted = jnp.zeros((k, b.shape[1]), F32)
    for j in range(8):
        start = pl.multiple_of(order[j] * k, k)
        fitted += blocks[j][pl.ds(start, k), :].astype(F32)
    fitted = fitted.astype(BF)
    total = jnp.zeros((rows, b.shape[2]), F32)
    for j in range(8):
        copies[j].wait()
        both = dot(jnp.concatenate([blocks[j][...], fitted], axis=0), b[j], NN)
        total += both[:rows]
        coulomb[order[j]] = both[rows:]
    for i in range(r):
        part = 2.0 * coulomb[i] - total[i * k : (i + 1) * k]
        out[i * k : (i + 1) * k, :] = part.astype(BF)


def fock_parts(place, blocks, b):
    r, _, n = b.shape
    rows = blocks[0].shape[0]
    return pl.pallas_call(
        fock_kernel,
        out_shape=array((rows, n), BF),
        in_specs=[SMEM] + [VMEM] * 8 + [HBM],
        out_specs=VMEM,
        scratch_shapes=[pltpu.VMEM((r, rows // r, n), F32)] + buffers(b),
        compiler_params=PARAMS,
    )(place, *blocks, b)


def owner_kernel(arrived, s0, s1, s2, s3, out, totals):
    total = (s0[...] + s1[...]) + (s2[...] + s3[...])
    size = totals.shape[0]
    totals[...] = total[:size]
    high, low = split(total[size:])
    tail = jnp.concatenate([high, low], axis=0).astype(BF)
    fock = arrived[0].astype(F32)
    for j in range(1, arrived.shape[0]):
        fock += arrived[j].astype(F32)
    fock = fock.astype(BF)
    rows = fock.shape[0]
    for p in range(out.shape[0]):
        for i in range(4):
            out[p, i * rows : (i + 1) * rows, :] = fock[:, i * 128 : (i + 1) * 128]
        out[p, 4 * rows :, :] = tail


def owner_sums(arrived, sums):
    copies, rows, _ = arrived.shape
    k = 2 * sums[0].shape[0] // 3
    return pl.pallas_call(
        owner_kernel,
        out_shape=(array((copies, 4 * rows + k, 128), BF), array((k, 128), F32)),
        in_specs=[VMEM] * 5,
        out_specs=(VMEM, VMEM),
        compiler_params=PARAMS,
    )(arrived, *sums)


def inverse_kernel(totals, out):
    size = 2 * totals.shape[0]
    half = unlanes(totals[...], 2)
    rows = lax.broadcasted_iota(jnp.int32, (size, 2 * size), 0)
    columns = lax.broadcasted_iota(jnp.int32, (size, 2 * size), 1)
    identity = (columns == rows + size).astype(F32)
    work = jnp.concatenate([half, identity[:, size:]], axis=1)
    for j in range(0, size, 2):
        first, second = work[j : j + 1], work[j + 1 : j + 2]
        aa, ab, bb = first[:, j : j + 1], first[:, j + 1 : j + 2], second[:, j + 1 : j + 2]
        scale = 1.0 / (aa * bb - ab * ab)
        top = (bb * scale) * first - (ab * scale) * second
        bottom = (aa * scale) * second - (ab * scale) * first
        rest = work - work[:, j : j + 1] * top - work[:, j + 1 : j + 2] * bottom
        work = jnp.where(rows == j, top, jnp.where(rows == j + 1, bottom, rest))
    out[...] = work[:, size:]


def inverse_of(totals):
    size = 2 * totals.shape[0]
    return pl.pallas_call(
        inverse_kernel,
        out_shape=array((size, size), F32),
        in_specs=[VMEM],
        out_specs=VMEM,
        compiler_params=PARAMS,
    )(totals)


def solve(pieces, inverse, k, rows):
    tail = jnp.zeros((k, 4 * k), F32)
    for j in range(pieces.shape[0]):
        tail += pieces[j, 4 * rows :, :].astype(F32)
    projected = unlanes(tail[: k // 2] + tail[k // 2 :], 4)
    return dot(inverse[...], projected, NN, HIGHEST)


def fock_rows(pieces, i, k, rows):
    per_row = k // rows
    parts = [lanes(pieces[i * per_row + h, : 4 * rows, :], 4) for h in range(per_row)]
    return jnp.concatenate(parts, axis=0).astype(F32)


def step_kernel(pieces, inverse, own, other, gap, out):
    r, k, _ = own.shape
    rows = (pieces.shape[1] - k) // 4
    high, low = split(solve(pieces, inverse, k, rows))
    high, low = high.astype(BF), low.astype(BF)
    for i in range(r):
        both = jnp.concatenate([own[i], other[i]], axis=0)
        mixed = dot(high, both, TN) + dot(low, both, TN)
        value = (mixed - fock_rows(pieces, i, k, rows)) / gap[i : i + 1, :]
        out[i] = value.astype(BF)


def step_update(pieces, inverse, own, other, gap):
    return pl.pallas_call(
        step_kernel,
        out_shape=array(own.shape, BF),
        in_specs=[VMEM] * 5,
        out_specs=VMEM,
        compiler_params=PARAMS,
    )(pieces, inverse, own, other, gap)


def last_kernel(place, pieces, inverse, own, other, gap, out, coupling):
    r, k, _ = own.shape
    rows = (pieces.shape[1] - k) // 4
    solved = solve(pieces, inverse, k, rows)
    turned = solved.T
    swapped = jnp.concatenate([turned[:, k:], turned[:, :k]], axis=1)
    coupling[...] = jnp.where(place[0] == 0, turned, swapped)
    high, low = split(solved)
    high, low = high.astype(BF), low.astype(BF)
    for i in range(r):
        both = jnp.concatenate([own[i], other[i]], axis=0)
        mixed = dot(high, both, TN) + dot(low, both, TN)
        value = (mixed - fock_rows(pieces, i, k, rows)) / gap[i : i + 1, :]
        out[:, i, :] = value


def last_update(place, pieces, inverse, own, other, gap):
    r, k, n = own.shape
    vectors, coupling = pl.pallas_call(
        last_kernel,
        out_shape=(array((k, r, n), F32), array((k, 2 * k), F32)),
        in_specs=[SMEM] + [VMEM] * 5,
        out_specs=(VMEM, VMEM),
        compiler_params=PARAMS,
    )(place, pieces, inverse, own, other, gap)
    return vectors, coupling.T


def ring(step):
    pairs = []
    for h in range(4):
        for c in range(2):
            way = step if c == 1 else -step
            pairs.append((2 * h + c, 2 * ((h + way) % 4) + c))
    return pairs


AHEAD = ring(1)
BACK = ring(-1)
SIBLING = [(i, i ^ 1) for i in range(8)]
OTHER = [(0, 1), (1, 0)]


def per_device(factors, trial_vectors, energy_gap):
    place = jnp.stack([lax.axis_index(a) for a in ("gx", "gy", "gz")])
    own = jnp.transpose(trial_vectors, (1, 0, 2)).astype(BF)
    b = pltpu.with_memory_space_constraint(jnp.transpose(factors, (1, 0, 2)), pltpu.HBM)

    def add(*terms):
        return sum(t.astype(F32) for t in terms).astype(BF)

    for iteration in range(ITERS):
        last = iteration == ITERS - 1
        theirs_far, mine_far = mix(place, own, b, (2,))
        theirs, *mine = mix(place, own, b, (-1, 1, 0))
        theirs_far = lax.ppermute(theirs_far, "gz", SIBLING)
        far = lax.ppermute(add(mine_far, theirs_far[0]), "gz", AHEAD)
        theirs = lax.ppermute(theirs, "gz", SIBLING)
        near = lax.ppermute(add(mine[0], theirs[0]), "gz", BACK)
        far = lax.ppermute(add(mine[1], theirs[1], far), "gz", AHEAD)
        first = add(mine[2], theirs[2], near, far)
        second = lax.ppermute(first, "gz", AHEAD)
        paired = lax.ppermute(first, "gz", SIBLING)
        third = lax.ppermute(first, "gz", BACK)
        fourth = lax.ppermute(second, "gz", AHEAD)
        other = lax.ppermute(own, "gx", OTHER)
        blocks = [first, second, third, fourth, paired]
        blocks += [lax.ppermute(a, "gz", SIBLING) for a in blocks[1:4]]
        fock = fock_parts(place, blocks, b)
        sums = local_sums(place, own, other, energy_gap, fock)
        arrived = lax.all_to_all(
            fock.reshape(16, -1, fock.shape[1]), "gy", 0, 0, tiled=True
        )
        sums = sums + lax.ppermute(sums, "gz", SIBLING)
        sums = [sums] + [
            lax.ppermute(sums, "gz", [(i, i ^ flip) for i in range(8)])
            for flip in (2, 4, 6)
        ]
        pieces, totals = owner_sums(arrived, sums)
        pieces = lax.all_to_all(pieces, "gy", 0, 0, tiled=True)
        inverse = inverse_of(totals)
        if last:
            return last_update(place, pieces, inverse, own, other, energy_gap)
        own = step_update(pieces, inverse, own, other, energy_gap)


def solution(mesh):
    placed = (P("gy", None, "gz"), P("gx", None, "gz"), P(None, "gz"))
    return jax.shard_map(
        per_device,
        mesh=mesh,
        in_specs=placed,
        out_specs=(P("gx", None, "gz"), P(None, "gx")),
        check_vma=False,
    )
```

time: 192 us -> 196 us (1.021)
  Pallas kernels: 33.2 us -> 48.1 us
  starting transfers between devices: 85 us -> 76.2 us
  local copies, waits for them, and re-layouts: 8.75 us -> 4.91 us
    pallas_call x9, Pallas kernels: 14.5 us -> 29.6 us  [the longest x4 15.7 us: mix(): pl.pallas_call(lambda *refs: mix_kernel(*refs, steps=steps), out_shape=ou...]
    ppermute x30 -> x32, waiting for transfers between devices: 53.2 us -> 64.4 us  [the longest x2 16.5 us: per_device(): near = lax.ppermute(add(mine[0], theirs[0]), 'gz', BACK)]
    ppermute x1 -> x2, waiting for transfers between devices: 5.26 us -> 0.01 us  [per_device(): other = lax.ppermute(own, 'gx', OTHER)]
    all_to_all x4, waiting for transfers between devices: 4.29 us -> 0.01 us  [the longest x2 0.01 us: per_device(): lax.all_to_all(fock.reshape(16, -1, fock.shape[1]), 'gy', 0, 0, tiled=True)]
    unnamed x20 -> x6, local copies, waits for them, and re-layouts: 8.75 us -> 4.91 us
    all_to_all x4, starting transfers between devices: 33.1 us -> 29.4 us  [the longest x2 14.9 us: per_device(): lax.all_to_all(fock.reshape(16, -1, fock.shape[1]), 'gy', 0, 0, tiled=True)]
    ppermute x1 -> x2, starting transfers between devices: 3.57 us -> 0.2 us  [per_device(): other = lax.ppermute(own, 'gx', OTHER)]
    ppermute x30 -> x32, starting transfers between devices: 48.3 us -> 46.6 us  [the longest x6 14.3 us: per_device(): lax.ppermute(sums, 'gz', [(i, i ^ flip) for i in range(8)])]
  transfers between devices with their start and end apart: 35 -> 38, of which waited for: 18 -> 16; matrix products, arithmetic and copies ran while one was open for 0% -> 0% of each run, Pallas kernels for 10% -> 19%
where the time goes in v1:
time: 196 us; the launch traced here: 195 us
  starting transfers between devices  76.2 us (39%)
  waiting for transfers between devices  64.4 us (33%)
  Pallas kernels  48.1 us (25%)
  local copies, waits for them, and re-layouts  4.91 us (3%)
    ppermute x2, waiting for transfers between devices, per_device(): near = lax.ppermute(add(mine[0], theirs[0]), 'gz', BACK)  16.5 us
    pallas_call x4, Pallas kernels, mix(): pl.pallas_call(lambda *refs: mix_kernel(*refs, steps=steps), out_shape=ou...  15.7 us
    all_to_all x2, starting transfers between devices, per_device(): lax.all_to_all(fock.reshape(16, -1, fock.shape[1]), 'gy', 0, 0, tiled=True)  14.9 us
    pallas_call x2, Pallas kernels, inverse_of(): pl.pallas_call(inverse_kernel, out_shape=array((size, size), F32), in_spe...  14.9 us
    all_to_all x2, starting transfers between devices, per_device(): pieces = lax.all_to_all(pieces, 'gy', 0, 0, tiled=True)  14.5 us
    ppermute x6, starting transfers between devices, per_device(): lax.ppermute(sums, 'gz', [(i, i ^ flip) for i in range(8)])  14.3 us
    ppermute x2, waiting for transfers between devices, per_device(): far = lax.ppermute(add(mine_far, theirs_far[0]), 'gz', AHEAD)  13.1 us
    ppermute x2, waiting for transfers between devices, per_device(): second = lax.ppermute(first, 'gz', AHEAD)  12.1 us
  transfers between devices with their start and end apart: 38, of which 16 were waited for; matrix products, arithmetic and copies ran while one was open for 0% of the time, Pallas kernels for 19%

profile of v1, /device:TPU:2, one launch (start us, length us, event | category | flops | bytes accessed | tf_op | source)
XLA Modules:
  0.0 195.1 jit_solution(2518232160828689683)
XLA Ops:
  0.6 4.6 %copy.11 = bf16[384,8,512]{2,0,1:T(8,128)(2,1)} copy(bf16[384,8,512]{2,1,0:T(8,128)(2,1)} %param.3) | data formatting | bytes 6291456 | tf_op args[0]
  5.3 0.3 copy.12
  5.6 3.8 %shard_map.51 = (bf16[1,256,384]{2,1,0:T(8,128)(2,1)S(1)}, f32[256,384]{1,0:T(8,128)S(1)}) custom-call(s32[3]{0:T(128)S(1)} %pad_add_fusion.refs_0_.place, bf16[8,32,512]{2,1,0:T(8,128)(2,1)S(1)} %bitcast.48, bf16[8,384,512]{2,1,0:T(8,128)(2,1)} %bitcast.53), custom_call_target="tpu_custom_call" | custom-call | tf_op jit(solution)/shard_map/pallas_call | solution.py:90
  9.5 4.0 %shard_map.50 = (bf16[3,256,384]{2,1,0:T(8,128)(2,1)S(1)}, f32[256,384]{1,0:T(8,128)S(1)}, f32[256,384]{1,0:T(8,128)S(1)}, f32[256,384]{1,0:T(8,128)S(1)}) custom-call(s32[3]{0:T(128)S(1)} %pad_add_fusion.refs_0_.place, bf16[8,32,512]{2,1,0:T(8,128)(2,1)S(1)} %bitcast.49, bf16[8,384,512]{2,1,0:T(8,128)(2,1)} %bitcast.54), custom_call_target="tpu_custom_call" | custom-call | tf_op jit(solution)/shard_map/pallas_call | solution.py:90
  13.6 0.6 collective-permute-start
  14.2 6.4 %collective-permute-start.3 = (bf16[256,384]{1,0:T(8,128)(2,1)S(1)}, bf16[256,384]{1,0:T(8,128)(2,1)S(1)}, u32[]{:S(2)}, u32[]{:S(2)}) collective-permute-start(bf16[256,384]{1,0:T(8,128)(2,1)S(1)} %fusion.7), channel_id=1, source_target_pairs={{0,6},{1,3},{2,0},{3,5},{4,2},{5,7},{6,4},{7,1},{8,14},{9,11},{10,... | collective-permute-start | bytes 589832 | tf_op jit(solution)/shard_map/ppermute | solution.py:314
  20.6 5.3 %collective-permute-done.3 = bf16[256,384]{1,0:T(8,128)(2,1)S(1)} collective-permute-done((bf16[256,384]{1,0:T(8,128)(2,1)S(1)}, bf16[256,384]{1,0:T(8,128)(2,1)S(1)}, u32[]{:S(2)}, u32[]{:S(2)}) %collective-permute-start.3) | collective-permute-done | bytes 196640 | tf_op jit(solution)/shard_map/ppermute | solution.py:314
  25.9 0.1 fusion.10
  26.0 2.0 %collective-permute-start.1 = (bf16[256,384]{1,0:T(8,128)(2,1)S(1)}, bf16[256,384]{1,0:T(8,128)(2,1)S(1)}, u32[]{:S(2)}, u32[]{:S(2)}) collective-permute-start(bf16[256,384]{1,0:T(8,128)(2,1)S(1)} %get-tuple-element.40), channel_id=1, source_target_pairs={{0,2},{1,7},{2,4},{3,1},{4,6},{5,3},{6,0},{7,5},{8,10},{9,15},{10,... | collective-permute-start | bytes 589832 | tf_op jit(solution)/shard_map/ppermute | solution.py:316
  28.0 2.8 %collective-permute-start.4 = (bf16[256,384]{1,0:T(8,128)(2,1)S(1)}, bf16[256,384]{1,0:T(8,128)(2,1)S(1)}, u32[]{:S(2)}, u32[]{:S(2)}) collective-permute-start(bf16[256,384]{1,0:T(8,128)(2,1)S(1)} %get-tuple-element.41), channel_id=1, source_target_pairs={{0,6},{1,3},{2,0},{3,5},{4,2},{5,7},{6,4},{7,1},{8,14},{9,11},{10,... | collective-permute-start | bytes 589832 | tf_op jit(solution)/shard_map/ppermute | solution.py:317
  30.8 9.0 %collective-permute-done.1 = bf16[256,384]{1,0:T(8,128)(2,1)S(1)} collective-permute-done((bf16[256,384]{1,0:T(8,128)(2,1)S(1)}, bf16[256,384]{1,0:T(8,128)(2,1)S(1)}, u32[]{:S(2)}, u32[]{:S(2)}) %collective-permute-start.1) | collective-permute-done | bytes 196640 | tf_op jit(solution)/shard_map/ppermute | solution.py:316
  39.8 0.1 fusion.13.refs_0_
  39.9 2.5 %collective-permute-start.5 = (bf16[256,384]{1,0:T(8,128)(2,1)S(1)}, bf16[256,384]{1,0:T(8,128)(2,1)S(1)}, u32[]{:S(2)}, u32[]{:S(2)}) collective-permute-start(bf16[256,384]{1,0:T(8,128)(2,1)S(1)} %fusion.13.refs_0_), channel_id=1, source_target_pairs={{0,6},{1,3},{2,0},{3,5},{4,2},{5,7},{6,4},{7,1},{8,14},{9,11},{10,... | collective-permute-start | bytes 589832 | tf_op jit(solution)/shard_map/ppermute | solution.py:319
  42.4 0.5 collective-permute-start.6
  42.9 5.8 %collective-permute-done.5.refs_1_ = bf16[256,384]{1,0:T(8,128)(2,1)S(1)} collective-permute-done((bf16[256,384]{1,0:T(8,128)(2,1)S(1)}, bf16[256,384]{1,0:T(8,128)(2,1)S(1)}, u32[]{:S(2)}, u32[]{:S(2)}) %collective-permute-start.5) | collective-permute-done | bytes 196640 | tf_op jit(solution)/shard_map/ppermute | solution.py:319
  48.7 3.1 %collective-permute-start.7 = (bf16[256,384]{1,0:T(8,128)(2,1)S(1)}, bf16[256,384]{1,0:T(8,128)(2,1)S(1)}, u32[]{:S(2)}, u32[]{:S(2)}) collective-permute-start(bf16[256,384]{1,0:T(8,128)(2,1)S(1)} %collective-permute-done.5.refs_1_), channel_id=1, source_target_pairs={{0,6},{1,3},{2,0},{3,5},{4,2},{5,7},{6,4},{7,1},{8,14},{9,11},{10,... | collective-permute-start | bytes 589832 | tf_op jit(solution)/shard_map/ppermute | solution.py:322
  51.8 0.5 collective-permute-start.9
  52.4 4.8 %collective-permute-done.7.refs_3_ = bf16[256,384]{1,0:T(8,128)(2,1)S(1)} collective-permute-done((bf16[256,384]{1,0:T(8,128)(2,1)S(1)}, bf16[256,384]{1,0:T(8,128)(2,1)S(1)}, u32[]{:S(2)}, u32[]{:S(2)}) %collective-permute-start.7) | collective-permute-done | bytes 196640 | tf_op jit(solution)/shard_map/ppermute | solution.py:322
  57.2 0.2 collective-permute-start.12
  57.4 1.2 collective-permute-done.11.refs_7_
  58.6 4.9 %shard_map.52.fock = bf16[256,512]{1,0:T(8,128)(2,1)} custom-call(s32[3]{0:T(128)S(1)} %pad_add_fusion.refs_0_.place, bf16[256,384]{1,0:T(8,128)(2,1)S(1)} %fusion.13.refs_0_, bf16[256,384]{1,0:T(8,128)(2,1)S(1)} %collective-permute-done.5.refs_1_, bf16[256,384]{1,0:T(8,128)(2,1)S(1)} %collective-permute-done.6.refs_2_, ...), custom_call_target="tpu_custom_call" | custom-call | tf_op jit(solution)/shard_map/pallas_call | solution.py:154
  63.5 8.2 %all-to-all-start = ((bf16[16,16,512]{2,1,0:T(8,128)(2,1)}), bf16[16,16,512]{2,1,0:T(8,128)(2,1)S(1)}, u32[]{:S(2)}, u32[]{:S(2)}) async-start(bf16[16,16,512]{2,1,0:T(8,128)(2,1)} %bitcast.9), calls=%async_computation | async-start | bytes 524288 | tf_op jit(solution)/shard_map/all_to_all | solution.py:328
  71.8 1.7 shard_map.53
  73.6 1.2 collective-permute-done.13
  74.8 1.9 collective-permute-start.14
  76.7 4.3 %collective-permute-start.15 = (f32[48,128]{1,0:T(8,128)S(1)}, f32[48,128]{1,0:T(8,128)S(1)}, u32[]{:S(2)}, u32[]{:S(2)}) collective-permute-start(f32[48,128]{1,0:T(8,128)S(1)} %add.55.s0), channel_id=1, source_target_pairs={{0,4},{1,5},{2,6},{3,7},{4,0},{5,1},{6,2},{7,3},{8,12},{9,13},{10,... | collective-permute-start | bytes 73736 | tf_op jit(solution)/shard_map/ppermute | solution.py:333
  81.0 0.3 collective-permute-start.16
  81.3 3.1 %collective-permute-done.15.s2 = f32[48,128]{1,0:T(8,128)S(1)} collective-permute-done((f32[48,128]{1,0:T(8,128)S(1)}, f32[48,128]{1,0:T(8,128)S(1)}, u32[]{:S(2)}, u32[]{:S(2)}) %collective-permute-start.15) | collective-permute-done | bytes 24608 | tf_op jit(solution)/shard_map/ppermute | solution.py:333
  84.4 2.5 %collective-permute-done.16.s3 = f32[48,128]{1,0:T(8,128)S(1)} collective-permute-done((f32[48,128]{1,0:T(8,128)S(1)}, f32[48,128]{1,0:T(8,128)S(1)}, u32[]{:S(2)}, u32[]{:S(2)}) %collective-permute-start.16) | collective-permute-done | bytes 24608 | tf_op jit(solution)/shard_map/ppermute | solution.py:333
  86.9 0.8 shard_map.54
  87.7 7.2 %all-to-all-start.1 = ((bf16[16,96,128]{2,1,0:T(8,128)(2,1)}), bf16[16,96,128]{2,1,0:T(8,128)(2,1)S(1)}, u32[]{:S(2)}, u32[]{:S(2)}) async-start(bf16[16,96,128]{2,1,0:T(8,128)(2,1)} %get-tuple-element.26), calls=%async_computation.1 | async-start | bytes 786432 | tf_op jit(solution)/shard_map/all_to_all | solution.py:337
  94.9 7.4 %shard_map.55.inverse = f32[64,64]{1,0:T(8,128)S(1)} custom-call(f32[32,128]{1,0:T(8,128)S(1)} %get-tuple-element.27.totals), custom_call_target="tpu_custom_call" | custom-call | tf_op jit(solution)/shard_map/pallas_call | solution.py:213
  102.4 0.6 shard_map.56.refs_1_.own
  103.0 3.8 %shard_map.58 = (bf16[1,256,384]{2,1,0:T(8,128)(2,1)S(1)}, f32[256,384]{1,0:T(8,128)S(1)}) custom-call(s32[3]{0:T(128)S(1)} %pad_add_fusion.refs_0_.place, bf16[8,32,512]{2,1,0:T(8,128)(2,1)S(1)} %shard_map.56.refs_1_.own, bf16[8,384,512]{2,1,0:T(8,128)(2,1)} %bitcast.56), custom_call_target="tpu_custom_call" | custom-call | tf_op jit(solution)/shard_map/pallas_call | solution.py:90
  106.9 4.0 %shard_map.57 = (bf16[3,256,384]{2,1,0:T(8,128)(2,1)S(1)}, f32[256,384]{1,0:T(8,128)S(1)}, f32[256,384]{1,0:T(8,128)S(1)}, f32[256,384]{1,0:T(8,128)S(1)}) custom-call(s32[3]{0:T(128)S(1)} %pad_add_fusion.refs_0_.place, bf16[8,32,512]{2,1,0:T(8,128)(2,1)S(1)} %shard_map.56.refs_1_.own, bf16[8,384,512]{2,1,0:T(8,128)(2,1)} %bitcast.57), custom_call_target="tpu_custom_call" | custom-call | tf_op jit(solution)/shard_map/pallas_call | solution.py:90
  111.0 0.6 collective-permute-start.17
  111.6 0.9 collective-permute-start.20
  112.5 7.8 %collective-permute-done.20 = bf16[256,384]{1,0:T(8,128)(2,1)S(1)} collective-permute-done((bf16[256,384]{1,0:T(8,128)(2,1)S(1)}, bf16[256,384]{1,0:T(8,128)(2,1)S(1)}, u32[]{:S(2)}, u32[]{:S(2)}) %collective-permute-start.20) | collective-permute-done | bytes 196640 | tf_op jit(solution)/shard_map/ppermute | solution.py:314
  120.4 0.1 fusion.3
  120.5 1.4 collective-permute-start.18
  121.9 2.8 %collective-permute-start.21 = (bf16[256,384]{1,0:T(8,128)(2,1)S(1)}, bf16[256,384]{1,0:T(8,128)(2,1)S(1)}, u32[]{:S(2)}, u32[]{:S(2)}) collective-permute-start(bf16[256,384]{1,0:T(8,128)(2,1)S(1)} %get-tuple-element.39), channel_id=1, source_target_pairs={{0,6},{1,3},{2,0},{3,5},{4,2},{5,7},{6,4},{7,1},{8,14},{9,11},{10,... | collective-permute-start | bytes 589832 | tf_op jit(solution)/shard_map/ppermute | solution.py:317
  124.7 7.5 %collective-permute-done.18 = bf16[256,384]{1,0:T(8,128)(2,1)S(1)} collective-permute-done((bf16[256,384]{1,0:T(8,128)(2,1)S(1)}, bf16[256,384]{1,0:T(8,128)(2,1)S(1)}, u32[]{:S(2)}, u32[]{:S(2)}) %collective-permute-start.18) | collective-permute-done | bytes 196640 | tf_op jit(solution)/shard_map/ppermute | solution.py:316
  132.2 0.1 fusion.6.refs_0_
  132.3 1.3 collective-permute-start.22
  133.6 2.0 %collective-permute-start.23 = (bf16[256,384]{1,0:T(8,128)(2,1)S(1)}, bf16[256,384]{1,0:T(8,128)(2,1)S(1)}, u32[]{:S(2)}, u32[]{:S(2)}) collective-permute-start(bf16[256,384]{1,0:T(8,128)(2,1)S(1)} %fusion.6.refs_0_), channel_id=1, source_target_pairs={{0,2},{1,7},{2,4},{3,1},{4,6},{5,3},{6,0},{7,5},{8,10},{9,15},{10,... | collective-permute-start | bytes 589832 | tf_op jit(solution)/shard_map/ppermute | solution.py:321
  135.5 6.3 %collective-permute-done.22.refs_1_ = bf16[256,384]{1,0:T(8,128)(2,1)S(1)} collective-permute-done((bf16[256,384]{1,0:T(8,128)(2,1)S(1)}, bf16[256,384]{1,0:T(8,128)(2,1)S(1)}, u32[]{:S(2)}, u32[]{:S(2)}) %collective-permute-start.22) | collective-permute-done | bytes 196640 | tf_op jit(solution)/shard_map/ppermute | solution.py:319
  141.8 3.7 %collective-permute-start.24 = (bf16[256,384]{1,0:T(8,128)(2,1)S(1)}, bf16[256,384]{1,0:T(8,128)(2,1)S(1)}, u32[]{:S(2)}, u32[]{:S(2)}) collective-permute-start(bf16[256,384]{1,0:T(8,128)(2,1)S(1)} %collective-permute-done.22.refs_1_), channel_id=1, source_target_pairs={{0,6},{1,3},{2,0},{3,5},{4,2},{5,7},{6,4},{7,1},{8,14},{9,11},{10,... | collective-permute-start | bytes 589832 | tf_op jit(solution)/shard_map/ppermute | solution.py:322
  145.5 0.5 collective-permute-start.26
  146.0 3.0 %collective-permute-done.24.refs_3_ = bf16[256,384]{1,0:T(8,128)(2,1)S(1)} collective-permute-done((bf16[256,384]{1,0:T(8,128)(2,1)S(1)}, bf16[256,384]{1,0:T(8,128)(2,1)S(1)}, u32[]{:S(2)}, u32[]{:S(2)}) %collective-permute-start.24) | collective-permute-done | bytes 196640 | tf_op jit(solution)/shard_map/ppermute | solution.py:322
  149.0 0.5 collective-permute-start.28
  149.5 1.0 collective-permute-done.28.refs_7_
  150.6 4.9 %shard_map.59.fock = bf16[256,512]{1,0:T(8,128)(2,1)} custom-call(s32[3]{0:T(128)S(1)} %pad_add_fusion.refs_0_.place, bf16[256,384]{1,0:T(8,128)(2,1)S(1)} %fusion.6.refs_0_, bf16[256,384]{1,0:T(8,128)(2,1)S(1)} %collective-permute-done.22.refs_1_, bf16[256,384]{1,0:T(8,128)(2,1)S(1)} %collective-permute-done.23.refs_2_, ...), custom_call_target="tpu_custom_call" | custom-call | tf_op jit(solution)/shard_map/pallas_call | solution.py:154
  155.5 6.7 %all-to-all-start.2 = ((bf16[16,16,512]{2,1,0:T(8,128)(2,1)}), bf16[16,16,512]{2,1,0:T(8,128)(2,1)S(1)}, u32[]{:S(2)}, u32[]{:S(2)}) async-start(bf16[16,16,512]{2,1,0:T(8,128)(2,1)} %bitcast.14), calls=%async_computation.2 | async-start | bytes 524288 | tf_op jit(solution)/shard_map/all_to_all | solution.py:328
  162.2 1.7 shard_map.60
  164.0 1.2 collective-permute-done.30
  165.2 4.1 %collective-permute-start.31 = (f32[48,128]{1,0:T(8,128)S(1)}, f32[48,128]{1,0:T(8,128)S(1)}, u32[]{:S(2)}, u32[]{:S(2)}) collective-permute-start(f32[48,128]{1,0:T(8,128)S(1)} %add.63.s0), channel_id=1, source_target_pairs={{0,2},{1,3},{2,0},{3,1},{4,6},{5,7},{6,4},{7,5},{8,10},{9,11},{10,... | collective-permute-start | bytes 73736 | tf_op jit(solution)/shard_map/ppermute | solution.py:333
  169.3 2.4 %collective-permute-start.32 = (f32[48,128]{1,0:T(8,128)S(1)}, f32[48,128]{1,0:T(8,128)S(1)}, u32[]{:S(2)}, u32[]{:S(2)}) collective-permute-start(f32[48,128]{1,0:T(8,128)S(1)} %add.63.s0), channel_id=1, source_target_pairs={{0,4},{1,5},{2,6},{3,7},{4,0},{5,1},{6,2},{7,3},{8,12},{9,13},{10,... | collective-permute-start | bytes 73736 | tf_op jit(solution)/shard_map/ppermute | solution.py:333
  171.7 1.3 collective-permute-start.33
  173.0 4.1 %collective-permute-done.32.s2 = f32[48,128]{1,0:T(8,128)S(1)} collective-permute-done((f32[48,128]{1,0:T(8,128)S(1)}, f32[48,128]{1,0:T(8,128)S(1)}, u32[]{:S(2)}, u32[]{:S(2)}) %collective-permute-start.32) | collective-permute-done | bytes 24608 | tf_op jit(solution)/shard_map/ppermute | solution.py:333
  177.1 0.6 collective-permute-done.33.s3
  177.7 0.8 shard_map.61
  178.5 7.2 %all-to-all-start.3 = ((bf16[16,96,128]{2,1,0:T(8,128)(2,1)}), bf16[16,96,128]{2,1,0:T(8,128)(2,1)S(1)}, u32[]{:S(2)}, u32[]{:S(2)}) async-start(bf16[16,96,128]{2,1,0:T(8,128)(2,1)} %get-tuple-element.34), calls=%async_computation.3 | async-start | bytes 786432 | tf_op jit(solution)/shard_map/all_to_all | solution.py:337
  185.7 7.4 %shard_map.62.inverse = f32[64,64]{1,0:T(8,128)S(1)} custom-call(f32[32,128]{1,0:T(8,128)S(1)} %get-tuple-element.35.totals), custom_call_target="tpu_custom_call" | custom-call | tf_op jit(solution)/shard_map/pallas_call | solution.py:213
  193.1 2.0 %shard_map.63 = (f32[32,8,512]{2,1,0:T(8,128)}, f32[32,64]{1,0:T(8,128)}) custom-call(s32[3]{0:T(128)S(1)} %pad_add_fusion.refs_0_.place, bf16[16,96,128]{2,1,0:T(8,128)(2,1)S(1)} %all-to-all-done.3.pieces, f32[64,64]{1,0:T(8,128)S(1)} %shard_map.62.inverse, bf16[8,32,512]{2,1,0:T(8,128)(2,1)S(1)} %shard_map.56.refs_1_.own, ...), custom_call_target="tpu_custom_call" | custom-call | tf_op jit(solution)/shard_map/pallas_call | solution.py:276
  (41 shorter events, 0.6 us)
Async XLA Ops:
  0.6 4.6 %copy-start.1 = (f32[32,8,512]{2,1,0:T(8,128)S(1)}, f32[32,8,512]{2,1,0:T(8,128)}, u32[]{:S(2)}) copy-start(f32[32,8,512]{2,1,0:T(8,128)} %param.4) | copy-start | bytes 1572868
  9.4 4.7 %collective-permute-start.2 = (bf16[1,256,384]{2,1,0:T(8,128)(2,1)S(1)}, bf16[1,256,384]{2,1,0:T(8,128)(2,1)S(1)}, u32[]{:S(2)}, u32[]{:S(2)}) collective-permute-start(bf16[1,256,384]{2,1,0:T(8,128)(2,1)S(1)} %get-tuple-element.25), channel_id=1, source_target_pairs={{0,1},{1,0},{2,3},{3,2},{4,5},{5,4},{6,7},{7,6},{8,9},{9,8},{10,11... | collective-permute-start | bytes 589832 | tf_op jit(solution)/shard_map/ppermute | solution.py:313
  13.6 12.3 %collective-permute-start = (bf16[3,256,384]{2,1,0:T(8,128)(2,1)S(1)}, bf16[3,256,384]{2,1,0:T(8,128)(2,1)S(1)}, u32[]{:S(2)}, u32[]{:S(2)}) collective-permute-start(bf16[3,256,384]{2,1,0:T(8,128)(2,1)S(1)} %get-tuple-element.21), channel_id=1, source_target_pairs={{0,1},{1,0},{2,3},{3,2},{4,5},{5,4},{6,7},{7,6},{8,9},{9,8},{10,11... | collective-permute-start | bytes 1769480 | tf_op jit(solution)/shard_map/ppermute | solution.py:315
  14.2 11.7 %collective-permute-start.3 = (bf16[256,384]{1,0:T(8,128)(2,1)S(1)}, bf16[256,384]{1,0:T(8,128)(2,1)S(1)}, u32[]{:S(2)}, u32[]{:S(2)}) collective-permute-start(bf16[256,384]{1,0:T(8,128)(2,1)S(1)} %fusion.7), channel_id=1, source_target_pairs={{0,6},{1,3},{2,0},{3,5},{4,2},{5,7},{6,4},{7,1},{8,14},{9,11},{10,... | collective-permute-start | bytes 589832 | tf_op jit(solution)/shard_map/ppermute | solution.py:314
  26.0 13.7 %collective-permute-start.1 = (bf16[256,384]{1,0:T(8,128)(2,1)S(1)}, bf16[256,384]{1,0:T(8,128)(2,1)S(1)}, u32[]{:S(2)}, u32[]{:S(2)}) collective-permute-start(bf16[256,384]{1,0:T(8,128)(2,1)S(1)} %get-tuple-element.40), channel_id=1, source_target_pairs={{0,2},{1,7},{2,4},{3,1},{4,6},{5,3},{6,0},{7,5},{8,10},{9,15},{10,... | collective-permute-start | bytes 589832 | tf_op jit(solution)/shard_map/ppermute | solution.py:316
  28.0 11.7 %collective-permute-start.4 = (bf16[256,384]{1,0:T(8,128)(2,1)S(1)}, bf16[256,384]{1,0:T(8,128)(2,1)S(1)}, u32[]{:S(2)}, u32[]{:S(2)}) collective-permute-start(bf16[256,384]{1,0:T(8,128)(2,1)S(1)} %get-tuple-element.41), channel_id=1, source_target_pairs={{0,6},{1,3},{2,0},{3,5},{4,2},{5,7},{6,4},{7,1},{8,14},{9,11},{10,... | collective-permute-start | bytes 589832 | tf_op jit(solution)/shard_map/ppermute | solution.py:317
  39.8 32.0 %copy-start = (f32[8,512]{1,0:T(8,128)S(1)}, f32[8,512]{1,0:T(8,128)}, u32[]{:S(2)}) copy-start(f32[8,512]{1,0:T(8,128)} %gap.7) | copy-start | bytes 49156
  39.9 8.8 %collective-permute-start.5 = (bf16[256,384]{1,0:T(8,128)(2,1)S(1)}, bf16[256,384]{1,0:T(8,128)(2,1)S(1)}, u32[]{:S(2)}, u32[]{:S(2)}) collective-permute-start(bf16[256,384]{1,0:T(8,128)(2,1)S(1)} %fusion.13.refs_0_), channel_id=1, source_target_pairs={{0,6},{1,3},{2,0},{3,5},{4,2},{5,7},{6,4},{7,1},{8,14},{9,11},{10,... | collective-permute-start | bytes 589832 | tf_op jit(solution)/shard_map/ppermute | solution.py:319
  42.4 10.0 %collective-permute-start.6 = (bf16[256,384]{1,0:T(8,128)(2,1)S(1)}, bf16[256,384]{1,0:T(8,128)(2,1)S(1)}, u32[]{:S(2)}, u32[]{:S(2)}) collective-permute-start(bf16[256,384]{1,0:T(8,128)(2,1)S(1)} %fusion.13.refs_0_), channel_id=1, source_target_pairs={{0,2},{1,7},{2,4},{3,1},{4,6},{5,3},{6,0},{7,5},{8,10},{9,15},{10,... | collective-permute-start | bytes 589832 | tf_op jit(solution)/shard_map/ppermute | solution.py:321
  48.7 8.5 %collective-permute-start.7 = (bf16[256,384]{1,0:T(8,128)(2,1)S(1)}, bf16[256,384]{1,0:T(8,128)(2,1)S(1)}, u32[]{:S(2)}, u32[]{:S(2)}) collective-permute-start(bf16[256,384]{1,0:T(8,128)(2,1)S(1)} %collective-permute-done.5.refs_1_), channel_id=1, source_target_pairs={{0,6},{1,3},{2,0},{3,5},{4,2},{5,7},{6,4},{7,1},{8,14},{9,11},{10,... | collective-permute-start | bytes 589832 | tf_op jit(solution)/shard_map/ppermute | solution.py:322
  51.8 5.5 %collective-permute-start.8 = (bf16[256,384]{1,0:T(8,128)(2,1)S(1)}, bf16[256,384]{1,0:T(8,128)(2,1)S(1)}, u32[]{:S(2)}, u32[]{:S(2)}) collective-permute-start(bf16[256,384]{1,0:T(8,128)(2,1)S(1)} %fusion.13.refs_0_), channel_id=1, source_target_pairs={{0,1},{1,0},{2,3},{3,2},{4,5},{5,4},{6,7},{7,6},{8,9},{9,8},{10,11... | collective-permute-start | bytes 589832 | tf_op jit(solution)/shard_map/ppermute | solution.py:320
  51.8 5.5 %collective-permute-start.9 = (bf16[256,384]{1,0:T(8,128)(2,1)S(1)}, bf16[256,384]{1,0:T(8,128)(2,1)S(1)}, u32[]{:S(2)}, u32[]{:S(2)}) collective-permute-start(bf16[256,384]{1,0:T(8,128)(2,1)S(1)} %collective-permute-done.5.refs_1_), channel_id=1, source_target_pairs={{0,1},{1,0},{2,3},{3,2},{4,5},{5,4},{6,7},{7,6},{8,9},{9,8},{10,11... | collective-permute-start | bytes 589832 | tf_op jit(solution)/shard_map/ppermute | solution.py:325
  52.4 5.0 %collective-permute-start.10 = (bf16[256,384]{1,0:T(8,128)(2,1)S(1)}, bf16[256,384]{1,0:T(8,128)(2,1)S(1)}, u32[]{:S(2)}, u32[]{:S(2)}) collective-permute-start(bf16[256,384]{1,0:T(8,128)(2,1)S(1)} %collective-permute-done.6.refs_2_), channel_id=1, source_target_pairs={{0,1},{1,0},{2,3},{3,2},{4,5},{5,4},{6,7},{7,6},{8,9},{9,8},{10,11... | collective-permute-start | bytes 589832 | tf_op jit(solution)/shard_map/ppermute | solution.py:325
  57.2 1.4 collective-permute-start.11
  57.2 14.6 %collective-permute-start.12 = (bf16[8,32,512]{2,1,0:T(8,128)(2,1)S(1)}, bf16[8,32,512]{2,1,0:T(8,128)(2,1)S(1)}, u32[]{:S(2)}, u32[]{:S(2)}) collective-permute-start(bf16[8,32,512]{2,1,0:T(8,128)(2,1)S(1)} %bitcast.50), channel_id=1, source_target_pairs={{0,128},{128,0},{1,129},{129,1},{2,130},{130,2},{3,131},{131,3},{4... | collective-permute-start | bytes 786440 | tf_op jit(solution)/shard_map/ppermute | solution.py:323
  63.5 23.4 %all-to-all-start = ((bf16[16,16,512]{2,1,0:T(8,128)(2,1)}), bf16[16,16,512]{2,1,0:T(8,128)(2,1)S(1)}, u32[]{:S(2)}, u32[]{:S(2)}) async-start(bf16[16,16,512]{2,1,0:T(8,128)(2,1)} %bitcast.9), calls=%async_computation | async-start | bytes 524288 | tf_op jit(solution)/shard_map/all_to_all | solution.py:328
  73.5 1.3 collective-permute-start.13
  74.8 6.5 %collective-permute-start.14 = (f32[48,128]{1,0:T(8,128)S(1)}, f32[48,128]{1,0:T(8,128)S(1)}, u32[]{:S(2)}, u32[]{:S(2)}) collective-permute-start(f32[48,128]{1,0:T(8,128)S(1)} %add.55.s0), channel_id=1, source_target_pairs={{0,2},{1,3},{2,0},{3,1},{4,6},{5,7},{6,4},{7,5},{8,10},{9,11},{10,... | collective-permute-start | bytes 73736 | tf_op jit(solution)/shard_map/ppermute | solution.py:333
  76.7 7.7 %collective-permute-start.15 = (f32[48,128]{1,0:T(8,128)S(1)}, f32[48,128]{1,0:T(8,128)S(1)}, u32[]{:S(2)}, u32[]{:S(2)}) collective-permute-start(f32[48,128]{1,0:T(8,128)S(1)} %add.55.s0), channel_id=1, source_target_pairs={{0,4},{1,5},{2,6},{3,7},{4,0},{5,1},{6,2},{7,3},{8,12},{9,13},{10,... | collective-permute-start | bytes 73736 | tf_op jit(solution)/shard_map/ppermute | solution.py:333
  81.0 5.9 %collective-permute-start.16 = (f32[48,128]{1,0:T(8,128)S(1)}, f32[48,128]{1,0:T(8,128)S(1)}, u32[]{:S(2)}, u32[]{:S(2)}) collective-permute-start(f32[48,128]{1,0:T(8,128)S(1)} %add.55.s0), channel_id=1, source_target_pairs={{0,6},{1,7},{2,4},{3,5},{4,2},{5,3},{6,0},{7,1},{8,14},{9,15},{10,... | collective-permute-start | bytes 73736 | tf_op jit(solution)/shard_map/ppermute | solution.py:333
  87.7 14.7 %all-to-all-start.1 = ((bf16[16,96,128]{2,1,0:T(8,128)(2,1)}), bf16[16,96,128]{2,1,0:T(8,128)(2,1)S(1)}, u32[]{:S(2)}, u32[]{:S(2)}) async-start(bf16[16,96,128]{2,1,0:T(8,128)(2,1)} %get-tuple-element.26), calls=%async_computation.1 | async-start | bytes 786432 | tf_op jit(solution)/shard_map/all_to_all | solution.py:337
  106.8 4.7 %collective-permute-start.19 = (bf16[1,256,384]{2,1,0:T(8,128)(2,1)S(1)}, bf16[1,256,384]{2,1,0:T(8,128)(2,1)S(1)}, u32[]{:S(2)}, u32[]{:S(2)}) collective-permute-start(bf16[1,256,384]{2,1,0:T(8,128)(2,1)S(1)} %get-tuple-element.33), channel_id=1, source_target_pairs={{0,1},{1,0},{2,3},{3,2},{4,5},{5,4},{6,7},{7,6},{8,9},{9,8},{10,11... | collective-permute-start | bytes 589832 | tf_op jit(solution)/shard_map/ppermute | solution.py:313
  111.0 9.4 %collective-permute-start.17 = (bf16[3,256,384]{2,1,0:T(8,128)(2,1)S(1)}, bf16[3,256,384]{2,1,0:T(8,128)(2,1)S(1)}, u32[]{:S(2)}, u32[]{:S(2)}) collective-permute-start(bf16[3,256,384]{2,1,0:T(8,128)(2,1)S(1)} %get-tuple-element.29), channel_id=1, source_target_pairs={{0,1},{1,0},{2,3},{3,2},{4,5},{5,4},{6,7},{7,6},{8,9},{9,8},{10,11... | collective-permute-start | bytes 1769480 | tf_op jit(solution)/shard_map/ppermute | solution.py:315
  111.6 8.8 %collective-permute-start.20 = (bf16[256,384]{1,0:T(8,128)(2,1)S(1)}, bf16[256,384]{1,0:T(8,128)(2,1)S(1)}, u32[]{:S(2)}, u32[]{:S(2)}) collective-permute-start(bf16[256,384]{1,0:T(8,128)(2,1)S(1)} %fusion), channel_id=1, source_target_pairs={{0,6},{1,3},{2,0},{3,5},{4,2},{5,7},{6,4},{7,1},{8,14},{9,11},{10,... | collective-permute-start | bytes 589832 | tf_op jit(solution)/shard_map/ppermute | solution.py:314
  120.5 11.7 %collective-permute-start.18 = (bf16[256,384]{1,0:T(8,128)(2,1)S(1)}, bf16[256,384]{1,0:T(8,128)(2,1)S(1)}, u32[]{:S(2)}, u32[]{:S(2)}) collective-permute-start(bf16[256,384]{1,0:T(8,128)(2,1)S(1)} %get-tuple-element.38), channel_id=1, source_target_pairs={{0,2},{1,7},{2,4},{3,1},{4,6},{5,3},{6,0},{7,5},{8,10},{9,15},{10,... | collective-permute-start | bytes 589832 | tf_op jit(solution)/shard_map/ppermute | solution.py:316
  121.9 10.3 %collective-permute-start.21 = (bf16[256,384]{1,0:T(8,128)(2,1)S(1)}, bf16[256,384]{1,0:T(8,128)(2,1)S(1)}, u32[]{:S(2)}, u32[]{:S(2)}) collective-permute-start(bf16[256,384]{1,0:T(8,128)(2,1)S(1)} %get-tuple-element.39), channel_id=1, source_target_pairs={{0,6},{1,3},{2,0},{3,5},{4,2},{5,7},{6,4},{7,1},{8,14},{9,11},{10,... | collective-permute-start | bytes 589832 | tf_op jit(solution)/shard_map/ppermute | solution.py:317
  132.3 9.5 %collective-permute-start.22 = (bf16[256,384]{1,0:T(8,128)(2,1)S(1)}, bf16[256,384]{1,0:T(8,128)(2,1)S(1)}, u32[]{:S(2)}, u32[]{:S(2)}) collective-permute-start(bf16[256,384]{1,0:T(8,128)(2,1)S(1)} %fusion.6.refs_0_), channel_id=1, source_target_pairs={{0,6},{1,3},{2,0},{3,5},{4,2},{5,7},{6,4},{7,1},{8,14},{9,11},{10,... | collective-permute-start | bytes 589832 | tf_op jit(solution)/shard_map/ppermute | solution.py:319
  133.6 12.4 %collective-permute-start.23 = (bf16[256,384]{1,0:T(8,128)(2,1)S(1)}, bf16[256,384]{1,0:T(8,128)(2,1)S(1)}, u32[]{:S(2)}, u32[]{:S(2)}) collective-permute-start(bf16[256,384]{1,0:T(8,128)(2,1)S(1)} %fusion.6.refs_0_), channel_id=1, source_target_pairs={{0,2},{1,7},{2,4},{3,1},{4,6},{5,3},{6,0},{7,5},{8,10},{9,15},{10,... | collective-permute-start | bytes 589832 | tf_op jit(solution)/shard_map/ppermute | solution.py:321
  141.8 7.2 %collective-permute-start.24 = (bf16[256,384]{1,0:T(8,128)(2,1)S(1)}, bf16[256,384]{1,0:T(8,128)(2,1)S(1)}, u32[]{:S(2)}, u32[]{:S(2)}) collective-permute-start(bf16[256,384]{1,0:T(8,128)(2,1)S(1)} %collective-permute-done.22.refs_1_), channel_id=1, source_target_pairs={{0,6},{1,3},{2,0},{3,5},{4,2},{5,7},{6,4},{7,1},{8,14},{9,11},{10,... | collective-permute-start | bytes 589832 | tf_op jit(solution)/shard_map/ppermute | solution.py:322
  145.5 4.0 %collective-permute-start.25 = (bf16[256,384]{1,0:T(8,128)(2,1)S(1)}, bf16[256,384]{1,0:T(8,128)(2,1)S(1)}, u32[]{:S(2)}, u32[]{:S(2)}) collective-permute-start(bf16[256,384]{1,0:T(8,128)(2,1)S(1)} %fusion.6.refs_0_), channel_id=1, source_target_pairs={{0,1},{1,0},{2,3},{3,2},{4,5},{5,4},{6,7},{7,6},{8,9},{9,8},{10,11... | collective-permute-start | bytes 589832 | tf_op jit(solution)/shard_map/ppermute | solution.py:320
  145.5 4.0 %collective-permute-start.26 = (bf16[256,384]{1,0:T(8,128)(2,1)S(1)}, bf16[256,384]{1,0:T(8,128)(2,1)S(1)}, u32[]{:S(2)}, u32[]{:S(2)}) collective-permute-start(bf16[256,384]{1,0:T(8,128)(2,1)S(1)} %collective-permute-done.22.refs_1_), channel_id=1, source_target_pairs={{0,1},{1,0},{2,3},{3,2},{4,5},{5,4},{6,7},{7,6},{8,9},{9,8},{10,11... | collective-permute-start | bytes 589832 | tf_op jit(solution)/shard_map/ppermute | solution.py:325
  146.0 3.5 %collective-permute-start.27 = (bf16[256,384]{1,0:T(8,128)(2,1)S(1)}, bf16[256,384]{1,0:T(8,128)(2,1)S(1)}, u32[]{:S(2)}, u32[]{:S(2)}) collective-permute-start(bf16[256,384]{1,0:T(8,128)(2,1)S(1)} %collective-permute-done.23.refs_2_), channel_id=1, source_target_pairs={{0,1},{1,0},{2,3},{3,2},{4,5},{5,4},{6,7},{7,6},{8,9},{9,8},{10,11... | collective-permute-start | bytes 589832 | tf_op jit(solution)/shard_map/ppermute | solution.py:325
  149.0 1.6 collective-permute-start.28
  149.5 12.7 %collective-permute-start.29 = (bf16[8,32,512]{2,1,0:T(8,128)(2,1)S(1)}, bf16[8,32,512]{2,1,0:T(8,128)(2,1)S(1)}, u32[]{:S(2)}, u32[]{:S(2)}) collective-permute-start(bf16[8,32,512]{2,1,0:T(8,128)(2,1)S(1)} %shard_map.56.refs_1_.own), channel_id=1, source_target_pairs={{0,128},{128,0},{1,129},{129,1},{2,130},{130,2},{3,131},{131,3},{4... | collective-permute-start | bytes 786440 | tf_op jit(solution)/shard_map/ppermute | solution.py:323
  155.5 22.2 %all-to-all-start.2 = ((bf16[16,16,512]{2,1,0:T(8,128)(2,1)}), bf16[16,16,512]{2,1,0:T(8,128)(2,1)S(1)}, u32[]{:S(2)}, u32[]{:S(2)}) async-start(bf16[16,16,512]{2,1,0:T(8,128)(2,1)} %bitcast.14), calls=%async_computation.2 | async-start | bytes 524288 | tf_op jit(solution)/shard_map/all_to_all | solution.py:328
  163.9 1.3 collective-permute-start.30
  165.2 7.8 %collective-permute-start.31 = (f32[48,128]{1,0:T(8,128)S(1)}, f32[48,128]{1,0:T(8,128)S(1)}, u32[]{:S(2)}, u32[]{:S(2)}) collective-permute-start(f32[48,128]{1,0:T(8,128)S(1)} %add.63.s0), channel_id=1, source_target_pairs={{0,2},{1,3},{2,0},{3,1},{4,6},{5,7},{6,4},{7,5},{8,10},{9,11},{10,... | collective-permute-start | bytes 73736 | tf_op jit(solution)/shard_map/ppermute | solution.py:333
  169.3 7.7 %collective-permute-start.32 = (f32[48,128]{1,0:T(8,128)S(1)}, f32[48,128]{1,0:T(8,128)S(1)}, u32[]{:S(2)}, u32[]{:S(2)}) collective-permute-start(f32[48,128]{1,0:T(8,128)S(1)} %add.63.s0), channel_id=1, source_target_pairs={{0,4},{1,5},{2,6},{3,7},{4,0},{5,1},{6,2},{7,3},{8,12},{9,13},{10,... | collective-permute-start | bytes 73736 | tf_op jit(solution)/shard_map/ppermute | solution.py:333
  171.7 5.9 %collective-permute-start.33 = (f32[48,128]{1,0:T(8,128)S(1)}, f32[48,128]{1,0:T(8,128)S(1)}, u32[]{:S(2)}, u32[]{:S(2)}) collective-permute-start(f32[48,128]{1,0:T(8,128)S(1)} %add.63.s0), channel_id=1, source_target_pairs={{0,6},{1,7},{2,4},{3,5},{4,2},{5,3},{6,0},{7,1},{8,14},{9,15},{10,... | collective-permute-start | bytes 73736 | tf_op jit(solution)/shard_map/ppermute | solution.py:333
  178.5 14.7 %all-to-all-start.3 = ((bf16[16,96,128]{2,1,0:T(8,128)(2,1)}), bf16[16,96,128]{2,1,0:T(8,128)(2,1)S(1)}, u32[]{:S(2)}, u32[]{:S(2)}) async-start(bf16[16,96,128]{2,1,0:T(8,128)(2,1)} %get-tuple-element.34), calls=%async_computation.3 | async-start | bytes 786432 | tf_op jit(solution)/shard_map/all_to_all | solution.py:337

commit v2 on v1

--- a/solution.py
+++ b/solution.py
@@ -66,35 +66,62 @@
     return [pltpu.VMEM(b.shape, b.dtype), pltpu.SemaphoreType.DMA((b.shape[0],))]
 
 
-def mix_kernel(place, x, source, *refs, steps):
-    *outs, b, arrivals = refs
-    copies = fetch(source, range(source.shape[0]), b, arrivals)
+def mix_kernel(place, x, held, source, *refs, steps):
+    *outs, streamed, arrivals = refs
+    copies = fetch(source, range(source.shape[0]), streamed, arrivals)
     rows = x.shape[1]
     count = len(steps)
     order = rows_of(steps, place[2], True) + rows_of(steps, place[2], False)
     chosen = jnp.concatenate([x[j] for j in order], axis=0)
-    for r in range(b.shape[0]):
-        copies[r].wait()
-        part = dot(chosen, b[r], NT)
+    middle = held.shape[1]
+
+    def put(r, columns, part):
         for j in range(count):
             theirs = part[j * rows : (j + 1) * rows]
-            outs[0][j, r * rows : (r + 1) * rows, :] = theirs.astype(BF)
+            outs[0][j, r * rows : (r + 1) * rows, columns] = theirs.astype(BF)
             mine = part[(count + j) * rows : (count + j + 1) * rows]
-            outs[1 + j][r * rows : (r + 1) * rows, :] = mine
+            outs[1 + j][r * rows : (r + 1) * rows, columns] = mine
+
+    for r in range(held.shape[0]):
+        put(r, slice(0, middle), dot(chosen, held[r], NT))
+    for r in range(held.shape[0]):
+        copies[r].wait()
+        put(r, slice(middle, outs[0].shape[2]), dot(chosen, streamed[r], NT))
 
 
 def mix(place, x, b, steps):
     r, k, _ = x.shape
-    shape = (r * k, b.shape[1])
+    shape = (r * k, b[0].shape[1] + b[1].shape[1])
     outs = [array((len(steps), *shape), BF)] + [array(shape, F32)] * len(steps)
     return pl.pallas_call(
         lambda *refs: mix_kernel(*refs, steps=steps),
         out_shape=outs,
-        in_specs=[SMEM, VMEM, HBM],
+        in_specs=[SMEM, VMEM, VMEM, HBM],
         out_specs=[VMEM] * len(outs),
-        scratch_shapes=buffers(b),
-        compiler_params=PARAMS,
-    )(place, x, b)
+        scratch_shapes=buffers(b[1]),
+        compiler_params=PARAMS,
+    )(place, x, *b)
+
+
+def add_kernel(mine, theirs, *refs):
+    *others, out = refs
+    total = mine[...] + theirs[0].astype(F32)
+    for other in others:
+        total += other[...].astype(F32)
+    out[...] = total.astype(BF)
+
+
+def add(mine, theirs, index, *others):
+    whole = pl.BlockSpec(mine.shape, lambda i: (0, 0))
+    return pl.pallas_call(
+        add_kernel,
+        grid=(1,),
+        out_shape=array(mine.shape, BF),
+        in_specs=[whole, pl.BlockSpec((1, *mine.shape), lambda i: (index, 0, 0))]
+        + [whole] * len(others),
+        out_specs=whole,
+        compiler_params=PARAMS,
+    )(mine, theirs, *others)
 
 
 def sums_kernel(place, own, other, gap, fock, message):
@@ -126,39 +153,46 @@
 
 def fock_kernel(place, *refs):
     blocks = refs[:8]
-    source, out, coulomb, b, arrivals = refs[8:]
+    held, source, out, coulomb, streamed, arrivals = refs[8:]
     r, k, _ = coulomb.shape
     rows = r * k
     got = (0, -1, 1, 2)
     order = rows_of(got, place[2], False) + rows_of(got, place[2], True)
-    copies = fetch(source, order, b, arrivals)
-    fitted = jnp.zeros((k, b.shape[1]), F32)
+    copies = fetch(source, order, streamed, arrivals)
+    fitted = jnp.zeros((k, blocks[0].shape[1]), F32)
     for j in range(8):
         start = pl.multiple_of(order[j] * k, k)
         fitted += blocks[j][pl.ds(start, k), :].astype(F32)
     fitted = fitted.astype(BF)
-    total = jnp.zeros((rows, b.shape[2]), F32)
+    middle = held.shape[1]
+    total = jnp.zeros((rows, held.shape[2]), F32)
+    for j in range(8):
+        left = jnp.concatenate([blocks[j][:, :middle], fitted[:, :middle]], axis=0)
+        both = dot(left, held[order[j]], NN)
+        total += both[:rows]
+        coulomb[order[j]] = both[rows:]
     for j in range(8):
         copies[j].wait()
-        both = dot(jnp.concatenate([blocks[j][...], fitted], axis=0), b[j], NN)
+        left = jnp.concatenate([blocks[j][:, middle:], fitted[:, middle:]], axis=0)
+        both = dot(left, streamed[j], NN)
         total += both[:rows]
-        coulomb[order[j]] = both[rows:]
+        coulomb[order[j]] += both[rows:]
     for i in range(r):
         part = 2.0 * coulomb[i] - total[i * k : (i + 1) * k]
         out[i * k : (i + 1) * k, :] = part.astype(BF)
 
 
 def fock_parts(place, blocks, b):
-    r, _, n = b.shape
+    r, _, n = b[0].shape
     rows = blocks[0].shape[0]
     return pl.pallas_call(
         fock_kernel,
         out_shape=array((rows, n), BF),
-        in_specs=[SMEM] + [VMEM] * 8 + [HBM],
+        in_specs=[SMEM] + [VMEM] * 9 + [HBM],
         out_specs=VMEM,
-        scratch_shapes=[pltpu.VMEM((r, rows // r, n), F32)] + buffers(b),
-        compiler_params=PARAMS,
-    )(place, *blocks, b)
+        scratch_shapes=[pltpu.VMEM((r, rows // r, n), F32)] + buffers(b[1]),
+        compiler_params=PARAMS,
+    )(place, *blocks, *b)
 
 
 def owner_kernel(arrived, s0, s1, s2, s3, out, totals):
@@ -301,21 +335,21 @@
 def per_device(factors, trial_vectors, energy_gap):
     place = jnp.stack([lax.axis_index(a) for a in ("gx", "gy", "gz")])
     own = jnp.transpose(trial_vectors, (1, 0, 2)).astype(BF)
-    b = pltpu.with_memory_space_constraint(jnp.transpose(factors, (1, 0, 2)), pltpu.HBM)
-
-    def add(*terms):
-        return sum(t.astype(F32) for t in terms).astype(BF)
+    middle = 2 * factors.shape[0] // 3
+    held = jnp.transpose(factors[:middle], (1, 0, 2))
+    streamed = jnp.transpose(factors[middle:], (1, 0, 2))
+    b = held, pltpu.with_memory_space_constraint(streamed, pltpu.HBM)
 
     for iteration in range(ITERS):
         last = iteration == ITERS - 1
         theirs_far, mine_far = mix(place, own, b, (2,))
         theirs, *mine = mix(place, own, b, (-1, 1, 0))
         theirs_far = lax.ppermute(theirs_far, "gz", SIBLING)
-        far = lax.ppermute(add(mine_far, theirs_far[0]), "gz", AHEAD)
+        far = lax.ppermute(add(mine_far, theirs_far, 0), "gz", AHEAD)
         theirs = lax.ppermute(theirs, "gz", SIBLING)
-        near = lax.ppermute(add(mine[0], theirs[0]), "gz", BACK)
-        far = lax.ppermute(add(mine[1], theirs[1], far), "gz", AHEAD)
-        first = add(mine[2], theirs[2], near, far)
+        near = lax.ppermute(add(mine[0], theirs, 0), "gz", BACK)
+        far = lax.ppermute(add(mine[1], theirs, 1, far), "gz", AHEAD)
+        first = add(mine[2], theirs, 2, near, far)
         second = lax.ppermute(first, "gz", AHEAD)
         paired = lax.ppermute(first, "gz", SIBLING)
         third = lax.ppermute(first, "gz", BACK)

time: 196 us -> 204 us (1.041)
  starting transfers between devices: 76.2 us -> 82.5 us
  local copies, waits for them, and re-layouts: 4.91 us -> 8.8 us
    ppermute x2, waiting for transfers between devices: 12.1 us -> 8.58 us  [per_device(): second = lax.ppermute(first, 'gz', AHEAD)]
    ppermute x2, starting transfers between devices: 2.46 us -> 5.62 us  [per_device(): third = lax.ppermute(first, 'gz', BACK)]
    slice x0 -> x3, local copies, waits for them, and re-layouts: none -> 3.07 us  [the longest x1 3.06 us: per_device(): held = jnp.transpose(factors[:middle], (1, 0, 2))]
    ppermute x2, starting transfers between devices: 0.2 us -> 3.03 us  [per_device(): other = lax.ppermute(own, 'gx', OTHER)]
    ppermute x2, waiting for transfers between devices: 0.01 us -> 2.14 us  [per_device(): theirs_far = lax.ppermute(theirs_far, 'gz', SIBLING)]
    ppermute x2, starting transfers between devices: 6.8 us -> 4.68 us  [per_device(): fourth = lax.ppermute(second, 'gz', AHEAD)]
    unnamed x6 -> x9, local copies, waits for them, and re-layouts: 4.91 us -> 5.73 us
  transfers between devices with their start and end apart: 38 -> 38, of which waited for: 16 -> 17; matrix products, arithmetic and copies ran while one was open for 0% -> 0% of each run, Pallas kernels for 19% -> 17%
where the time goes in v2:
time: 204 us
  starting transfers between devices  82.5 us (40%)
  waiting for transfers between devices  64.2 us (31%)
  Pallas kernels  47.2 us (23%)
  local copies, waits for them, and re-layouts  8.8 us (4%)
    ppermute x2, waiting for transfers between devices, per_device(): far = lax.ppermute(add(mine_far, theirs_far, 0), 'gz', AHEAD)  18 us
    pallas_call x4, Pallas kernels, mix(): pl.pallas_call(lambda *refs: mix_kernel(*refs, steps=steps), out_shape=ou...  15.7 us
    ppermute x6, starting transfers between devices, per_device(): lax.ppermute(sums, 'gz', [(i, i ^ flip) for i in range(8)])  14.9 us
    pallas_call x2, Pallas kernels, inverse_of(): pl.pallas_call(inverse_kernel, out_shape=array((size, size), F32), in_spe...  14.9 us
    all_to_all x2, starting transfers between devices, per_device(): lax.all_to_all(fock.reshape(16, -1, fock.shape[1]), 'gy', 0, 0, tiled=True)  14.8 us
    all_to_all x2, starting transfers between devices, per_device(): pieces = lax.all_to_all(pieces, 'gy', 0, 0, tiled=True)  14.5 us
    ppermute x2, waiting for transfers between devices, per_device(): far = lax.ppermute(add(mine[1], theirs, 1, far), 'gz', AHEAD)  12.4 us
    ppermute x6, waiting for transfers between devices, per_device(): lax.ppermute(sums, 'gz', [(i, i ^ flip) for i in range(8)])  9.96 us
  transfers between devices with their start and end apart: 38, of which 17 were waited for; matrix products, arithmetic and copies ran while one was open for 0% of the time, Pallas kernels for 17%

profile of v2, /device:TPU:2, one launch (start us, length us, event | category | flops | bytes accessed | tf_op | source)
XLA Modules:
  0.0 203.7 jit_solution(12662457141881058491)
XLA Ops:
  0.6 3.1 %slice.6 = bf16[256,8,512]{2,1,0:T(8,128)(2,1)} slice(bf16[384,8,512]{2,1,0:T(8,128)(2,1)} %param.3), slice={[0:256], [0:8], [0:512]} | slice | bytes 4194304 | tf_op jit(solution)/shard_map/slice | solution.py:339
  3.7 1.0 copy-done.2
  4.7 0.3 copy.17
  5.0 2.3 %copy.15 = bf16[256,8,512]{2,0,1:T(8,128)(2,1)S(1)} copy(bf16[256,8,512]{2,1,0:T(8,128)(2,1)} %slice.6) | data formatting | bytes 4194304
  7.4 1.3 copy.16
  8.8 4.2 %shard_map.50 = (bf16[3,256,384]{2,1,0:T(8,128)(2,1)S(1)}, f32[256,384]{1,0:T(8,128)S(1)}, f32[256,384]{1,0:T(8,128)S(1)}, f32[256,384]{1,0:T(8,128)S(1)}) custom-call(s32[3]{0:T(128)S(1)} %pad_add_fusion.refs_0_.place, bf16[8,32,512]{2,1,0:T(8,128)(2,1)S(1)} %bitcast.21, bf16[8,256,512]{2,1,0:T(8,128)(2,1)S(1)} %bitcast.15, bf16[8,128,512]{2,1,0:T(8,128)(2,1)} %bitcast.26), custom_call_target="tpu_custom_call" | custom-call | tf_op jit(solution)/shard_map/pallas_call | solution.py:96
  12.9 0.1 collective-permute-start
  13.0 3.7 %shard_map.52 = (bf16[1,256,384]{2,1,0:T(8,128)(2,1)S(1)}, f32[256,384]{1,0:T(8,128)S(1)}) custom-call(s32[3]{0:T(128)S(1)} %pad_add_fusion.refs_0_.place, bf16[8,32,512]{2,1,0:T(8,128)(2,1)S(1)} %bitcast.22, bf16[8,256,512]{2,1,0:T(8,128)(2,1)S(1)} %bitcast.16, bf16[8,128,512]{2,1,0:T(8,128)(2,1)} %bitcast.27), custom_call_target="tpu_custom_call" | custom-call | tf_op jit(solution)/shard_map/pallas_call | solution.py:96
  16.8 0.6 collective-permute-start.2
  17.3 1.1 collective-permute-done.2.theirs
  18.4 6.4 %collective-permute-start.3 = (bf16[256,384]{1,0:T(8,128)(2,1)S(1)}, bf16[256,384]{1,0:T(8,128)(2,1)S(1)}, u32[]{:S(2)}, u32[]{:S(2)}) collective-permute-start(bf16[256,384]{1,0:T(8,128)(2,1)S(1)} %shard_map.53), channel_id=1, source_target_pairs={{0,6},{1,3},{2,0},{3,5},{4,2},{5,7},{6,4},{7,1},{8,14},{9,11},{10,... | collective-permute-start | bytes 589832 | tf_op jit(solution)/shard_map/ppermute | solution.py:348
  25.0 9.0 %collective-permute-done.3.refs_0_ = bf16[256,384]{1,0:T(8,128)(2,1)S(1)} collective-permute-done((bf16[256,384]{1,0:T(8,128)(2,1)S(1)}, bf16[256,384]{1,0:T(8,128)(2,1)S(1)}, u32[]{:S(2)}, u32[]{:S(2)}) %collective-permute-start.3) | collective-permute-done | bytes 196640 | tf_op jit(solution)/shard_map/ppermute | solution.py:348
  34.0 4.6 %collective-permute-start.4 = (bf16[256,384]{1,0:T(8,128)(2,1)S(1)}, bf16[256,384]{1,0:T(8,128)(2,1)S(1)}, u32[]{:S(2)}, u32[]{:S(2)}) collective-permute-start(bf16[256,384]{1,0:T(8,128)(2,1)S(1)} %shard_map.54), channel_id=1, source_target_pairs={{0,6},{1,3},{2,0},{3,5},{4,2},{5,7},{6,4},{7,1},{8,14},{9,11},{10,... | collective-permute-start | bytes 589832 | tf_op jit(solution)/shard_map/ppermute | solution.py:351
  38.6 4.9 %collective-permute-done.4.refs_1_ = bf16[256,384]{1,0:T(8,128)(2,1)S(1)} collective-permute-done((bf16[256,384]{1,0:T(8,128)(2,1)S(1)}, bf16[256,384]{1,0:T(8,128)(2,1)S(1)}, u32[]{:S(2)}, u32[]{:S(2)}) %collective-permute-start.4) | collective-permute-done | bytes 196640 | tf_op jit(solution)/shard_map/ppermute | solution.py:351
  43.5 0.1 shard_map.55.refs_0_
  43.6 4.7 %collective-permute-start.5 = (bf16[256,384]{1,0:T(8,128)(2,1)S(1)}, bf16[256,384]{1,0:T(8,128)(2,1)S(1)}, u32[]{:S(2)}, u32[]{:S(2)}) collective-permute-start(bf16[256,384]{1,0:T(8,128)(2,1)S(1)} %shard_map.55.refs_0_), channel_id=1, source_target_pairs={{0,6},{1,3},{2,0},{3,5},{4,2},{5,7},{6,4},{7,1},{8,14},{9,11},{10,... | collective-permute-start | bytes 589832 | tf_op jit(solution)/shard_map/ppermute | solution.py:353
  48.4 3.2 %collective-permute-done.5.refs_1_ = bf16[256,384]{1,0:T(8,128)(2,1)S(1)} collective-permute-done((bf16[256,384]{1,0:T(8,128)(2,1)S(1)}, bf16[256,384]{1,0:T(8,128)(2,1)S(1)}, u32[]{:S(2)}, u32[]{:S(2)}) %collective-permute-start.5) | collective-permute-done | bytes 196640 | tf_op jit(solution)/shard_map/ppermute | solution.py:353
  51.6 4.5 %collective-permute-start.7 = (bf16[256,384]{1,0:T(8,128)(2,1)S(1)}, bf16[256,384]{1,0:T(8,128)(2,1)S(1)}, u32[]{:S(2)}, u32[]{:S(2)}) collective-permute-start(bf16[256,384]{1,0:T(8,128)(2,1)S(1)} %collective-permute-done.5.refs_1_), channel_id=1, source_target_pairs={{0,6},{1,3},{2,0},{3,5},{4,2},{5,7},{6,4},{7,1},{8,14},{9,11},{10,... | collective-permute-start | bytes 589832 | tf_op jit(solution)/shard_map/ppermute | solution.py:356
  56.2 0.5 collective-permute-start.9
  56.7 2.7 %collective-permute-done.7.refs_3_ = bf16[256,384]{1,0:T(8,128)(2,1)S(1)} collective-permute-done((bf16[256,384]{1,0:T(8,128)(2,1)S(1)}, bf16[256,384]{1,0:T(8,128)(2,1)S(1)}, u32[]{:S(2)}, u32[]{:S(2)}) %collective-permute-start.7) | collective-permute-done | bytes 196640 | tf_op jit(solution)/shard_map/ppermute | solution.py:356
  59.3 1.5 collective-permute-start.11
  60.8 3.0 %collective-permute-start.12 = (bf16[8,32,512]{2,1,0:T(8,128)(2,1)S(1)}, bf16[8,32,512]{2,1,0:T(8,128)(2,1)S(1)}, u32[]{:S(2)}, u32[]{:S(2)}) collective-permute-start(bf16[8,32,512]{2,1,0:T(8,128)(2,1)S(1)} %bitcast.23), channel_id=1, source_target_pairs={{0,128},{128,0},{1,129},{129,1},{2,130},{130,2},{3,131},{131,3},{4... | collective-permute-start | bytes 786440 | tf_op jit(solution)/shard_map/ppermute | solution.py:357
  63.9 4.6 %shard_map.56.fock = bf16[256,512]{1,0:T(8,128)(2,1)} custom-call(s32[3]{0:T(128)S(1)} %pad_add_fusion.refs_0_.place, bf16[256,384]{1,0:T(8,128)(2,1)S(1)} %shard_map.55.refs_0_, bf16[256,384]{1,0:T(8,128)(2,1)S(1)} %collective-permute-done.5.refs_1_, bf16[256,384]{1,0:T(8,128)(2,1)S(1)} %collective-permute-done.6.refs_2_, ...), custom_call_target="tpu_custom_call" | custom-call | tf_op jit(solution)/shard_map/pallas_call | solution.py:188
  68.5 7.5 %all-to-all-start = ((bf16[16,16,512]{2,1,0:T(8,128)(2,1)}), bf16[16,16,512]{2,1,0:T(8,128)(2,1)S(1)}, u32[]{:S(2)}, u32[]{:S(2)}) async-start(bf16[16,16,512]{2,1,0:T(8,128)(2,1)} %bitcast.6), calls=%async_computation | async-start | bytes 524288 | tf_op jit(solution)/shard_map/all_to_all | solution.py:362
  76.0 1.7 shard_map.57
  77.8 1.2 collective-permute-done.13
  79.0 1.4 collective-permute-start.14
  80.4 5.1 %collective-permute-start.15 = (f32[48,128]{1,0:T(8,128)S(1)}, f32[48,128]{1,0:T(8,128)S(1)}, u32[]{:S(2)}, u32[]{:S(2)}) collective-permute-start(f32[48,128]{1,0:T(8,128)S(1)} %add.6.s0), channel_id=1, source_target_pairs={{0,4},{1,5},{2,6},{3,7},{4,0},{5,1},{6,2},{7,3},{8,12},{9,13},{10,... | collective-permute-start | bytes 73736 | tf_op jit(solution)/shard_map/ppermute | solution.py:367
  85.5 2.6 %collective-permute-done.15.s2 = f32[48,128]{1,0:T(8,128)S(1)} collective-permute-done((f32[48,128]{1,0:T(8,128)S(1)}, f32[48,128]{1,0:T(8,128)S(1)}, u32[]{:S(2)}, u32[]{:S(2)}) %collective-permute-start.15) | collective-permute-done | bytes 24608 | tf_op jit(solution)/shard_map/ppermute | solution.py:367
  88.1 3.3 %collective-permute-done.16.s3 = f32[48,128]{1,0:T(8,128)S(1)} collective-permute-done((f32[48,128]{1,0:T(8,128)S(1)}, f32[48,128]{1,0:T(8,128)S(1)}, u32[]{:S(2)}, u32[]{:S(2)}) %collective-permute-start.16) | collective-permute-done | bytes 24608 | tf_op jit(solution)/shard_map/ppermute | solution.py:367
  91.5 0.7 copy-done
  92.2 7.2 %all-to-all-start.1 = ((bf16[16,96,128]{2,1,0:T(8,128)(2,1)}), bf16[16,96,128]{2,1,0:T(8,128)(2,1)S(1)}, u32[]{:S(2)}, u32[]{:S(2)}) async-start(bf16[16,96,128]{2,1,0:T(8,128)(2,1)} %copy-done), calls=%async_computation.1 | async-start | bytes 786432 | tf_op jit(solution)/shard_map/all_to_all | solution.py:371
  99.4 7.4 %shard_map.59.inverse = f32[64,64]{1,0:T(8,128)S(1)} custom-call(f32[32,128]{1,0:T(8,128)S(1)} %get-tuple-element.27.totals), custom_call_target="tpu_custom_call" | custom-call | tf_op jit(solution)/shard_map/pallas_call | solution.py:247
  106.9 0.6 shard_map.60.refs_1_.own
  107.5 4.2 %shard_map.61 = (bf16[3,256,384]{2,1,0:T(8,128)(2,1)S(1)}, f32[256,384]{1,0:T(8,128)S(1)}, f32[256,384]{1,0:T(8,128)S(1)}, f32[256,384]{1,0:T(8,128)S(1)}) custom-call(s32[3]{0:T(128)S(1)} %pad_add_fusion.refs_0_.place, bf16[8,32,512]{2,1,0:T(8,128)(2,1)S(1)} %shard_map.60.refs_1_.own, bf16[8,256,512]{2,1,0:T(8,128)(2,1)S(1)} %bitcast.18, ...), custom_call_target="tpu_custom_call" | custom-call | tf_op jit(solution)/shard_map/pallas_call | solution.py:96
  111.7 0.1 collective-permute-start.17
  111.8 3.7 %shard_map.63 = (bf16[1,256,384]{2,1,0:T(8,128)(2,1)S(1)}, f32[256,384]{1,0:T(8,128)S(1)}) custom-call(s32[3]{0:T(128)S(1)} %pad_add_fusion.refs_0_.place, bf16[8,32,512]{2,1,0:T(8,128)(2,1)S(1)} %shard_map.60.refs_1_.own, bf16[8,256,512]{2,1,0:T(8,128)(2,1)S(1)} %bitcast.19, bf16[8,128,512]{2,1,0:T(8,128)(2,1)} %bitcast.30), custom_call_target="tpu_custom_call" | custom-call | tf_op jit(solution)/shard_map/pallas_call | solution.py:96
  115.5 0.6 collective-permute-start.19
  116.1 1.1 collective-permute-done.19.theirs
  117.2 1.1 collective-permute-start.20
  118.4 1.9 collective-permute-start.18
  120.3 9.0 %collective-permute-done.20.refs_0_ = bf16[256,384]{1,0:T(8,128)(2,1)S(1)} collective-permute-done((bf16[256,384]{1,0:T(8,128)(2,1)S(1)}, bf16[256,384]{1,0:T(8,128)(2,1)S(1)}, u32[]{:S(2)}, u32[]{:S(2)}) %collective-permute-start.20) | collective-permute-done | bytes 196640 | tf_op jit(solution)/shard_map/ppermute | solution.py:348
  129.4 1.7 collective-permute-start.21
  131.1 7.5 %collective-permute-done.21.refs_1_ = bf16[256,384]{1,0:T(8,128)(2,1)S(1)} collective-permute-done((bf16[256,384]{1,0:T(8,128)(2,1)S(1)}, bf16[256,384]{1,0:T(8,128)(2,1)S(1)}, u32[]{:S(2)}, u32[]{:S(2)}) %collective-permute-start.21) | collective-permute-done | bytes 196640 | tf_op jit(solution)/shard_map/ppermute | solution.py:351
  138.6 0.1 shard_map.66.refs_0_
  138.6 0.5 collective-permute-start.22
  139.1 5.6 %collective-permute-start.23 = (bf16[256,384]{1,0:T(8,128)(2,1)S(1)}, bf16[256,384]{1,0:T(8,128)(2,1)S(1)}, u32[]{:S(2)}, u32[]{:S(2)}) collective-permute-start(bf16[256,384]{1,0:T(8,128)(2,1)S(1)} %shard_map.66.refs_0_), channel_id=1, source_target_pairs={{0,2},{1,7},{2,4},{3,1},{4,6},{5,3},{6,0},{7,5},{8,10},{9,15},{10,... | collective-permute-start | bytes 589832 | tf_op jit(solution)/shard_map/ppermute | solution.py:355
  144.8 5.3 %collective-permute-done.22.refs_1_ = bf16[256,384]{1,0:T(8,128)(2,1)S(1)} collective-permute-done((bf16[256,384]{1,0:T(8,128)(2,1)S(1)}, bf16[256,384]{1,0:T(8,128)(2,1)S(1)}, u32[]{:S(2)}, u32[]{:S(2)}) %collective-permute-start.22) | collective-permute-done | bytes 196640 | tf_op jit(solution)/shard_map/ppermute | solution.py:353
  150.1 0.1 collective-permute-start.24
  150.2 0.5 collective-permute-start.26
  150.7 0.2 collective-permute-done.23.refs_2_
  150.9 6.4 %collective-permute-done.24.refs_3_ = bf16[256,384]{1,0:T(8,128)(2,1)S(1)} collective-permute-done((bf16[256,384]{1,0:T(8,128)(2,1)S(1)}, bf16[256,384]{1,0:T(8,128)(2,1)S(1)}, u32[]{:S(2)}, u32[]{:S(2)}) %collective-permute-start.24) | collective-permute-done | bytes 196640 | tf_op jit(solution)/shard_map/ppermute | solution.py:356
  157.4 1.4 collective-permute-done.28.refs_7_
  158.8 4.6 %shard_map.67.fock = bf16[256,512]{1,0:T(8,128)(2,1)} custom-call(s32[3]{0:T(128)S(1)} %pad_add_fusion.refs_0_.place, bf16[256,384]{1,0:T(8,128)(2,1)S(1)} %shard_map.66.refs_0_, bf16[256,384]{1,0:T(8,128)(2,1)S(1)} %collective-permute-done.22.refs_1_, bf16[256,384]{1,0:T(8,128)(2,1)S(1)} %collective-permute-done.23.refs_2_, ...), custom_call_target="tpu_custom_call" | custom-call | tf_op jit(solution)/shard_map/pallas_call | solution.py:188
  163.4 7.3 %all-to-all-start.2 = ((bf16[16,16,512]{2,1,0:T(8,128)(2,1)}), bf16[16,16,512]{2,1,0:T(8,128)(2,1)S(1)}, u32[]{:S(2)}, u32[]{:S(2)}) async-start(bf16[16,16,512]{2,1,0:T(8,128)(2,1)} %bitcast.7), calls=%async_computation.2 | async-start | bytes 524288 | tf_op jit(solution)/shard_map/all_to_all | solution.py:362
  170.7 1.7 shard_map.68
  172.6 1.2 collective-permute-done.30
  173.7 4.7 %collective-permute-start.31 = (f32[48,128]{1,0:T(8,128)S(1)}, f32[48,128]{1,0:T(8,128)S(1)}, u32[]{:S(2)}, u32[]{:S(2)}) collective-permute-start(f32[48,128]{1,0:T(8,128)S(1)} %add.7.s0), channel_id=1, source_target_pairs={{0,2},{1,3},{2,0},{3,1},{4,6},{5,7},{6,4},{7,5},{8,10},{9,11},{10,... | collective-permute-start | bytes 73736 | tf_op jit(solution)/shard_map/ppermute | solution.py:367
  178.5 3.7 %collective-permute-start.33 = (f32[48,128]{1,0:T(8,128)S(1)}, f32[48,128]{1,0:T(8,128)S(1)}, u32[]{:S(2)}, u32[]{:S(2)}) collective-permute-start(f32[48,128]{1,0:T(8,128)S(1)} %add.7.s0), channel_id=1, source_target_pairs={{0,6},{1,7},{2,4},{3,5},{4,2},{5,3},{6,0},{7,1},{8,14},{9,15},{10,... | collective-permute-start | bytes 73736 | tf_op jit(solution)/shard_map/ppermute | solution.py:367
  182.1 4.1 %collective-permute-done.32.s2 = f32[48,128]{1,0:T(8,128)S(1)} collective-permute-done((f32[48,128]{1,0:T(8,128)S(1)}, f32[48,128]{1,0:T(8,128)S(1)}, u32[]{:S(2)}, u32[]{:S(2)}) %collective-permute-start.32) | collective-permute-done | bytes 24608 | tf_op jit(solution)/shard_map/ppermute | solution.py:367
  186.2 0.8 shard_map.69
  187.0 7.2 %all-to-all-start.3 = ((bf16[16,96,128]{2,1,0:T(8,128)(2,1)}), bf16[16,96,128]{2,1,0:T(8,128)(2,1)S(1)}, u32[]{:S(2)}, u32[]{:S(2)}) async-start(bf16[16,96,128]{2,1,0:T(8,128)(2,1)} %get-tuple-element.34), calls=%async_computation.3 | async-start | bytes 786432 | tf_op jit(solution)/shard_map/all_to_all | solution.py:371
  194.2 7.4 %shard_map.70.inverse = f32[64,64]{1,0:T(8,128)S(1)} custom-call(f32[32,128]{1,0:T(8,128)S(1)} %get-tuple-element.35.totals), custom_call_target="tpu_custom_call" | custom-call | tf_op jit(solution)/shard_map/pallas_call | solution.py:247
  201.7 2.0 shard_map.71
  (49 shorter events, 0.8 us)
Async XLA Ops:
  3.7 1.0 copy-start.2
  5.0 2.4 %slice-start = ((bf16[384,8,512]{2,1,0:T(8,128)(2,1)}), bf16[128,8,512]{2,1,0:T(8,128)(2,1)S(1)}, s32[]{:S(2)}) async-start(bf16[384,8,512]{2,1,0:T(8,128)(2,1)} %param.3), calls=%async_computation.4 | async-start | bytes 2097152 | tf_op jit(solution)/shard_map/slice | solution.py:340
  12.9 11.9 %collective-permute-start = (bf16[3,256,384]{2,1,0:T(8,128)(2,1)S(1)}, bf16[3,256,384]{2,1,0:T(8,128)(2,1)S(1)}, u32[]{:S(2)}, u32[]{:S(2)}) collective-permute-start(bf16[3,256,384]{2,1,0:T(8,128)(2,1)S(1)} %get-tuple-element.21), channel_id=1, source_target_pairs={{0,1},{1,0},{2,3},{3,2},{4,5},{5,4},{6,7},{7,6},{8,9},{9,8},{10,11... | collective-permute-start | bytes 1769480 | tf_op jit(solution)/shard_map/ppermute | solution.py:349
  16.8 1.7 collective-permute-start.2
  18.4 15.5 %collective-permute-start.3 = (bf16[256,384]{1,0:T(8,128)(2,1)S(1)}, bf16[256,384]{1,0:T(8,128)(2,1)S(1)}, u32[]{:S(2)}, u32[]{:S(2)}) collective-permute-start(bf16[256,384]{1,0:T(8,128)(2,1)S(1)} %shard_map.53), channel_id=1, source_target_pairs={{0,6},{1,3},{2,0},{3,5},{4,2},{5,7},{6,4},{7,1},{8,14},{9,11},{10,... | collective-permute-start | bytes 589832 | tf_op jit(solution)/shard_map/ppermute | solution.py:348
  24.9 13.8 %collective-permute-start.1 = (bf16[256,384]{1,0:T(8,128)(2,1)S(1)}, bf16[256,384]{1,0:T(8,128)(2,1)S(1)}, u32[]{:S(2)}, u32[]{:S(2)}) collective-permute-start(bf16[256,384]{1,0:T(8,128)(2,1)S(1)} %shard_map.51), channel_id=1, source_target_pairs={{0,2},{1,7},{2,4},{3,1},{4,6},{5,3},{6,0},{7,5},{8,10},{9,15},{10,... | collective-permute-start | bytes 589832 | tf_op jit(solution)/shard_map/ppermute | solution.py:350
  34.0 9.5 %collective-permute-start.4 = (bf16[256,384]{1,0:T(8,128)(2,1)S(1)}, bf16[256,384]{1,0:T(8,128)(2,1)S(1)}, u32[]{:S(2)}, u32[]{:S(2)}) collective-permute-start(bf16[256,384]{1,0:T(8,128)(2,1)S(1)} %shard_map.54), channel_id=1, source_target_pairs={{0,6},{1,3},{2,0},{3,5},{4,2},{5,7},{6,4},{7,1},{8,14},{9,11},{10,... | collective-permute-start | bytes 589832 | tf_op jit(solution)/shard_map/ppermute | solution.py:351
  43.6 32.4 %copy-start.1 = (f32[8,512]{1,0:T(8,128)S(1)}, f32[8,512]{1,0:T(8,128)}, u32[]{:S(2)}) copy-start(f32[8,512]{1,0:T(8,128)} %gap.7) | copy-start | bytes 49156
  43.6 8.0 %collective-permute-start.5 = (bf16[256,384]{1,0:T(8,128)(2,1)S(1)}, bf16[256,384]{1,0:T(8,128)(2,1)S(1)}, u32[]{:S(2)}, u32[]{:S(2)}) collective-permute-start(bf16[256,384]{1,0:T(8,128)(2,1)S(1)} %shard_map.55.refs_0_), channel_id=1, source_target_pairs={{0,6},{1,3},{2,0},{3,5},{4,2},{5,7},{6,4},{7,1},{8,14},{9,11},{10,... | collective-permute-start | bytes 589832 | tf_op jit(solution)/shard_map/ppermute | solution.py:353
  48.4 8.3 %collective-permute-start.6 = (bf16[256,384]{1,0:T(8,128)(2,1)S(1)}, bf16[256,384]{1,0:T(8,128)(2,1)S(1)}, u32[]{:S(2)}, u32[]{:S(2)}) collective-permute-start(bf16[256,384]{1,0:T(8,128)(2,1)S(1)} %shard_map.55.refs_0_), channel_id=1, source_target_pairs={{0,2},{1,7},{2,4},{3,1},{4,6},{5,3},{6,0},{7,5},{8,10},{9,15},{10,... | collective-permute-start | bytes 589832 | tf_op jit(solution)/shard_map/ppermute | solution.py:355
  51.6 7.7 %collective-permute-start.7 = (bf16[256,384]{1,0:T(8,128)(2,1)S(1)}, bf16[256,384]{1,0:T(8,128)(2,1)S(1)}, u32[]{:S(2)}, u32[]{:S(2)}) collective-permute-start(bf16[256,384]{1,0:T(8,128)(2,1)S(1)} %collective-permute-done.5.refs_1_), channel_id=1, source_target_pairs={{0,6},{1,3},{2,0},{3,5},{4,2},{5,7},{6,4},{7,1},{8,14},{9,11},{10,... | collective-permute-start | bytes 589832 | tf_op jit(solution)/shard_map/ppermute | solution.py:356
  56.2 7.7 %collective-permute-start.8 = (bf16[256,384]{1,0:T(8,128)(2,1)S(1)}, bf16[256,384]{1,0:T(8,128)(2,1)S(1)}, u32[]{:S(2)}, u32[]{:S(2)}) collective-permute-start(bf16[256,384]{1,0:T(8,128)(2,1)S(1)} %shard_map.55.refs_0_), channel_id=1, source_target_pairs={{0,1},{1,0},{2,3},{3,2},{4,5},{5,4},{6,7},{7,6},{8,9},{9,8},{10,11... | collective-permute-start | bytes 589832 | tf_op jit(solution)/shard_map/ppermute | solution.py:354
  56.2 7.7 %collective-permute-start.9 = (bf16[256,384]{1,0:T(8,128)(2,1)S(1)}, bf16[256,384]{1,0:T(8,128)(2,1)S(1)}, u32[]{:S(2)}, u32[]{:S(2)}) collective-permute-start(bf16[256,384]{1,0:T(8,128)(2,1)S(1)} %collective-permute-done.5.refs_1_), channel_id=1, source_target_pairs={{0,1},{1,0},{2,3},{3,2},{4,5},{5,4},{6,7},{7,6},{8,9},{9,8},{10,11... | collective-permute-start | bytes 589832 | tf_op jit(solution)/shard_map/ppermute | solution.py:359
  56.7 7.2 %collective-permute-start.10 = (bf16[256,384]{1,0:T(8,128)(2,1)S(1)}, bf16[256,384]{1,0:T(8,128)(2,1)S(1)}, u32[]{:S(2)}, u32[]{:S(2)}) collective-permute-start(bf16[256,384]{1,0:T(8,128)(2,1)S(1)} %collective-permute-done.6.refs_2_), channel_id=1, source_target_pairs={{0,1},{1,0},{2,3},{3,2},{4,5},{5,4},{6,7},{7,6},{8,9},{9,8},{10,11... | collective-permute-start | bytes 589832 | tf_op jit(solution)/shard_map/ppermute | solution.py:359
  59.3 4.5 %collective-permute-start.11 = (bf16[256,384]{1,0:T(8,128)(2,1)S(1)}, bf16[256,384]{1,0:T(8,128)(2,1)S(1)}, u32[]{:S(2)}, u32[]{:S(2)}) collective-permute-start(bf16[256,384]{1,0:T(8,128)(2,1)S(1)} %collective-permute-done.7.refs_3_), channel_id=1, source_target_pairs={{0,1},{1,0},{2,3},{3,2},{4,5},{5,4},{6,7},{7,6},{8,9},{9,8},{10,11... | collective-permute-start | bytes 589832 | tf_op jit(solution)/shard_map/ppermute | solution.py:359
  60.8 15.2 %collective-permute-start.12 = (bf16[8,32,512]{2,1,0:T(8,128)(2,1)S(1)}, bf16[8,32,512]{2,1,0:T(8,128)(2,1)S(1)}, u32[]{:S(2)}, u32[]{:S(2)}) collective-permute-start(bf16[8,32,512]{2,1,0:T(8,128)(2,1)S(1)} %bitcast.23), channel_id=1, source_target_pairs={{0,128},{128,0},{1,129},{129,1},{2,130},{130,2},{3,131},{131,3},{4... | collective-permute-start | bytes 786440 | tf_op jit(solution)/shard_map/ppermute | solution.py:357
  68.5 22.9 %all-to-all-start = ((bf16[16,16,512]{2,1,0:T(8,128)(2,1)}), bf16[16,16,512]{2,1,0:T(8,128)(2,1)S(1)}, u32[]{:S(2)}, u32[]{:S(2)}) async-start(bf16[16,16,512]{2,1,0:T(8,128)(2,1)} %bitcast.6), calls=%async_computation | async-start | bytes 524288 | tf_op jit(solution)/shard_map/all_to_all | solution.py:362
  77.7 1.3 collective-permute-start.13
  79.0 6.5 %collective-permute-start.14 = (f32[48,128]{1,0:T(8,128)S(1)}, f32[48,128]{1,0:T(8,128)S(1)}, u32[]{:S(2)}, u32[]{:S(2)}) collective-permute-start(f32[48,128]{1,0:T(8,128)S(1)} %add.6.s0), channel_id=1, source_target_pairs={{0,2},{1,3},{2,0},{3,1},{4,6},{5,7},{6,4},{7,5},{8,10},{9,11},{10,... | collective-permute-start | bytes 73736 | tf_op jit(solution)/shard_map/ppermute | solution.py:367
  80.4 7.7 %collective-permute-start.15 = (f32[48,128]{1,0:T(8,128)S(1)}, f32[48,128]{1,0:T(8,128)S(1)}, u32[]{:S(2)}, u32[]{:S(2)}) collective-permute-start(f32[48,128]{1,0:T(8,128)S(1)} %add.6.s0), channel_id=1, source_target_pairs={{0,4},{1,5},{2,6},{3,7},{4,0},{5,1},{6,2},{7,3},{8,12},{9,13},{10,... | collective-permute-start | bytes 73736 | tf_op jit(solution)/shard_map/ppermute | solution.py:367
  85.5 5.9 %collective-permute-start.16 = (f32[48,128]{1,0:T(8,128)S(1)}, f32[48,128]{1,0:T(8,128)S(1)}, u32[]{:S(2)}, u32[]{:S(2)}) collective-permute-start(f32[48,128]{1,0:T(8,128)S(1)} %add.6.s0), channel_id=1, source_target_pairs={{0,6},{1,7},{2,4},{3,5},{4,2},{5,3},{6,0},{7,1},{8,14},{9,15},{10,... | collective-permute-start | bytes 73736 | tf_op jit(solution)/shard_map/ppermute | solution.py:367
  91.5 0.7 copy-start
  92.2 14.7 %all-to-all-start.1 = ((bf16[16,96,128]{2,1,0:T(8,128)(2,1)}), bf16[16,96,128]{2,1,0:T(8,128)(2,1)S(1)}, u32[]{:S(2)}, u32[]{:S(2)}) async-start(bf16[16,96,128]{2,1,0:T(8,128)(2,1)} %copy-done), calls=%async_computation.1 | async-start | bytes 786432 | tf_op jit(solution)/shard_map/all_to_all | solution.py:371
  111.7 6.6 %collective-permute-start.17 = (bf16[3,256,384]{2,1,0:T(8,128)(2,1)S(1)}, bf16[3,256,384]{2,1,0:T(8,128)(2,1)S(1)}, u32[]{:S(2)}, u32[]{:S(2)}) collective-permute-start(bf16[3,256,384]{2,1,0:T(8,128)(2,1)S(1)} %get-tuple-element.29), channel_id=1, source_target_pairs={{0,1},{1,0},{2,3},{3,2},{4,5},{5,4},{6,7},{7,6},{8,9},{9,8},{10,11... | collective-permute-start | bytes 1769480 | tf_op jit(solution)/shard_map/ppermute | solution.py:349
  115.5 1.7 collective-permute-start.19
  117.2 12.2 %collective-permute-start.20 = (bf16[256,384]{1,0:T(8,128)(2,1)S(1)}, bf16[256,384]{1,0:T(8,128)(2,1)S(1)}, u32[]{:S(2)}, u32[]{:S(2)}) collective-permute-start(bf16[256,384]{1,0:T(8,128)(2,1)S(1)} %shard_map.64), channel_id=1, source_target_pairs={{0,6},{1,3},{2,0},{3,5},{4,2},{5,7},{6,4},{7,1},{8,14},{9,11},{10,... | collective-permute-start | bytes 589832 | tf_op jit(solution)/shard_map/ppermute | solution.py:348
  118.4 12.7 %collective-permute-start.18 = (bf16[256,384]{1,0:T(8,128)(2,1)S(1)}, bf16[256,384]{1,0:T(8,128)(2,1)S(1)}, u32[]{:S(2)}, u32[]{:S(2)}) collective-permute-start(bf16[256,384]{1,0:T(8,128)(2,1)S(1)} %shard_map.62), channel_id=1, source_target_pairs={{0,2},{1,7},{2,4},{3,1},{4,6},{5,3},{6,0},{7,5},{8,10},{9,15},{10,... | collective-permute-start | bytes 589832 | tf_op jit(solution)/shard_map/ppermute | solution.py:350
  129.4 9.2 %collective-permute-start.21 = (bf16[256,384]{1,0:T(8,128)(2,1)S(1)}, bf16[256,384]{1,0:T(8,128)(2,1)S(1)}, u32[]{:S(2)}, u32[]{:S(2)}) collective-permute-start(bf16[256,384]{1,0:T(8,128)(2,1)S(1)} %shard_map.65), channel_id=1, source_target_pairs={{0,6},{1,3},{2,0},{3,5},{4,2},{5,7},{6,4},{7,1},{8,14},{9,11},{10,... | collective-permute-start | bytes 589832 | tf_op jit(solution)/shard_map/ppermute | solution.py:351
  138.6 11.5 %collective-permute-start.22 = (bf16[256,384]{1,0:T(8,128)(2,1)S(1)}, bf16[256,384]{1,0:T(8,128)(2,1)S(1)}, u32[]{:S(2)}, u32[]{:S(2)}) collective-permute-start(bf16[256,384]{1,0:T(8,128)(2,1)S(1)} %shard_map.66.refs_0_), channel_id=1, source_target_pairs={{0,6},{1,3},{2,0},{3,5},{4,2},{5,7},{6,4},{7,1},{8,14},{9,11},{10,... | collective-permute-start | bytes 589832 | tf_op jit(solution)/shard_map/ppermute | solution.py:353
  139.1 11.8 %collective-permute-start.23 = (bf16[256,384]{1,0:T(8,128)(2,1)S(1)}, bf16[256,384]{1,0:T(8,128)(2,1)S(1)}, u32[]{:S(2)}, u32[]{:S(2)}) collective-permute-start(bf16[256,384]{1,0:T(8,128)(2,1)S(1)} %shard_map.66.refs_0_), channel_id=1, source_target_pairs={{0,2},{1,7},{2,4},{3,1},{4,6},{5,3},{6,0},{7,5},{8,10},{9,15},{10,... | collective-permute-start | bytes 589832 | tf_op jit(solution)/shard_map/ppermute | solution.py:355
  150.1 7.3 %collective-permute-start.24 = (bf16[256,384]{1,0:T(8,128)(2,1)S(1)}, bf16[256,384]{1,0:T(8,128)(2,1)S(1)}, u32[]{:S(2)}, u32[]{:S(2)}) collective-permute-start(bf16[256,384]{1,0:T(8,128)(2,1)S(1)} %collective-permute-done.22.refs_1_), channel_id=1, source_target_pairs={{0,6},{1,3},{2,0},{3,5},{4,2},{5,7},{6,4},{7,1},{8,14},{9,11},{10,... | collective-permute-start | bytes 589832 | tf_op jit(solution)/shard_map/ppermute | solution.py:356
  150.2 7.2 %collective-permute-start.25 = (bf16[256,384]{1,0:T(8,128)(2,1)S(1)}, bf16[256,384]{1,0:T(8,128)(2,1)S(1)}, u32[]{:S(2)}, u32[]{:S(2)}) collective-permute-start(bf16[256,384]{1,0:T(8,128)(2,1)S(1)} %shard_map.66.refs_0_), channel_id=1, source_target_pairs={{0,1},{1,0},{2,3},{3,2},{4,5},{5,4},{6,7},{7,6},{8,9},{9,8},{10,11... | collective-permute-start | bytes 589832 | tf_op jit(solution)/shard_map/ppermute | solution.py:354
  150.2 7.2 %collective-permute-start.26 = (bf16[256,384]{1,0:T(8,128)(2,1)S(1)}, bf16[256,384]{1,0:T(8,128)(2,1)S(1)}, u32[]{:S(2)}, u32[]{:S(2)}) collective-permute-start(bf16[256,384]{1,0:T(8,128)(2,1)S(1)} %collective-permute-done.22.refs_1_), channel_id=1, source_target_pairs={{0,1},{1,0},{2,3},{3,2},{4,5},{5,4},{6,7},{7,6},{8,9},{9,8},{10,11... | collective-permute-start | bytes 589832 | tf_op jit(solution)/shard_map/ppermute | solution.py:359
  150.9 6.5 %collective-permute-start.27 = (bf16[256,384]{1,0:T(8,128)(2,1)S(1)}, bf16[256,384]{1,0:T(8,128)(2,1)S(1)}, u32[]{:S(2)}, u32[]{:S(2)}) collective-permute-start(bf16[256,384]{1,0:T(8,128)(2,1)S(1)} %collective-permute-done.23.refs_2_), channel_id=1, source_target_pairs={{0,1},{1,0},{2,3},{3,2},{4,5},{5,4},{6,7},{7,6},{8,9},{9,8},{10,11... | collective-permute-start | bytes 589832 | tf_op jit(solution)/shard_map/ppermute | solution.py:359
  157.4 1.4 collective-permute-start.28
  157.4 13.3 %collective-permute-start.29 = (bf16[8,32,512]{2,1,0:T(8,128)(2,1)S(1)}, bf16[8,32,512]{2,1,0:T(8,128)(2,1)S(1)}, u32[]{:S(2)}, u32[]{:S(2)}) collective-permute-start(bf16[8,32,512]{2,1,0:T(8,128)(2,1)S(1)} %shard_map.60.refs_1_.own), channel_id=1, source_target_pairs={{0,128},{128,0},{1,129},{129,1},{2,130},{130,2},{3,131},{131,3},{4... | collective-permute-start | bytes 786440 | tf_op jit(solution)/shard_map/ppermute | solution.py:357
  163.4 22.8 %all-to-all-start.2 = ((bf16[16,16,512]{2,1,0:T(8,128)(2,1)}), bf16[16,16,512]{2,1,0:T(8,128)(2,1)S(1)}, u32[]{:S(2)}, u32[]{:S(2)}) async-start(bf16[16,16,512]{2,1,0:T(8,128)(2,1)} %bitcast.7), calls=%async_computation.2 | async-start | bytes 524288 | tf_op jit(solution)/shard_map/all_to_all | solution.py:362
  172.5 1.3 collective-permute-start.30
  173.7 8.4 %collective-permute-start.31 = (f32[48,128]{1,0:T(8,128)S(1)}, f32[48,128]{1,0:T(8,128)S(1)}, u32[]{:S(2)}, u32[]{:S(2)}) collective-permute-start(f32[48,128]{1,0:T(8,128)S(1)} %add.7.s0), channel_id=1, source_target_pairs={{0,2},{1,3},{2,0},{3,1},{4,6},{5,7},{6,4},{7,5},{8,10},{9,11},{10,... | collective-permute-start | bytes 73736 | tf_op jit(solution)/shard_map/ppermute | solution.py:367
  178.5 7.7 %collective-permute-start.32 = (f32[48,128]{1,0:T(8,128)S(1)}, f32[48,128]{1,0:T(8,128)S(1)}, u32[]{:S(2)}, u32[]{:S(2)}) collective-permute-start(f32[48,128]{1,0:T(8,128)S(1)} %add.7.s0), channel_id=1, source_target_pairs={{0,4},{1,5},{2,6},{3,7},{4,0},{5,1},{6,2},{7,3},{8,12},{9,13},{10,... | collective-permute-start | bytes 73736 | tf_op jit(solution)/shard_map/ppermute | solution.py:367
  178.5 7.7 %collective-permute-start.33 = (f32[48,128]{1,0:T(8,128)S(1)}, f32[48,128]{1,0:T(8,128)S(1)}, u32[]{:S(2)}, u32[]{:S(2)}) collective-permute-start(f32[48,128]{1,0:T(8,128)S(1)} %add.7.s0), channel_id=1, source_target_pairs={{0,6},{1,7},{2,4},{3,5},{4,2},{5,3},{6,0},{7,1},{8,14},{9,15},{10,... | collective-permute-start | bytes 73736 | tf_op jit(solution)/shard_map/ppermute | solution.py:367
  187.0 14.7 %all-to-all-start.3 = ((bf16[16,96,128]{2,1,0:T(8,128)(2,1)}), bf16[16,96,128]{2,1,0:T(8,128)(2,1)S(1)}, u32[]{:S(2)}, u32[]{:S(2)}) async-start(bf16[16,96,128]{2,1,0:T(8,128)(2,1)} %get-tuple-element.34), calls=%async_computation.3 | async-start | bytes 786432 | tf_op jit(solution)/shard_map/all_to_all | solution.py:371
